TPU v7x, 32 devices: a 4x4x1 block of a 4x4x8 slice. The times are simulated.
32 devices in a mesh: replica: 1 (over z), model: 32 (over y, x, core).
Axes of the slice: x: 4, y: 4, z: 1, core: 2. Of those that a mesh axis runs over, the one named last changes fastest.
The devices are a block of a 4x4x8 slice.
Arguments:
- hidden: bfloat16 [2048, 8192], P('replica')
- w_query: bfloat16 [8192, 8192], P(None, 'model')
- w_key: bfloat16 [8192, 128], replicated
- w_value: bfloat16 [8192, 128], replicated
- w_out: bfloat16 [8192, 8192], P('model')
- key_cache: bfloat16 [2048, 512, 128], P(('replica', 'model'))
- value_cache: bfloat16 [2048, 512, 128], P(('replica', 'model'))
- lengths: int32 [2048], P('replica')
Outputs:
- output 1: bfloat16 [2048, 8192], P('replica')
- output 2: bfloat16 [2048, 512, 128], P(('replica', 'model'))
- output 3: bfloat16 [2048, 512, 128], P(('replica', 'model'))
All inputs are finite; a program needn't handle non-finite values.
Results may differ from a plain program's by a relative error of at most 0.0109961.
Values are sent between devices in bfloat16 or wider.
A program may use at most 768 MiB of HBM per device.

v0:
```python
import math
import jax
import jax.numpy as jnp
from jax import lax
from jax.sharding import PartitionSpec as P


def attend_row(row_args):
    query_row, key_row, value_row, row_len = row_args
    seq_len, head_dim = key_row.shape
    n_heads = query_row.shape[0]
    block_len = math.gcd(seq_len, 512)
    score_scale = head_dim ** -0.5

    def block_step(block_idx, loop_state):
        run_max, run_sum, ctx_acc = loop_state
        block_start = block_idx * block_len
        key_block = lax.dynamic_slice_in_dim(key_row, block_start, block_len, 0)
        value_block = lax.dynamic_slice_in_dim(value_row, block_start, block_len, 0)
        scores = jnp.einsum('hd,td->ht', query_row, key_block, preferred_element_type=jnp.float32) * score_scale
        positions = block_start + lax.broadcasted_iota(jnp.int32, (1, block_len), 1)
        scores = jnp.where(positions <= row_len, scores, -jnp.inf)
        new_max = jnp.maximum(run_max, jnp.max(scores, axis=1))
        weights = jnp.exp(scores - new_max[:, None])
        rescale = jnp.exp(run_max - new_max)
        run_sum = rescale * run_sum + jnp.sum(weights, axis=1)
        ctx_acc = rescale[:, None] * ctx_acc + jnp.einsum('ht,td->hd', weights.astype(jnp.bfloat16), value_block, preferred_element_type=jnp.float32)
        return new_max, run_sum, ctx_acc

    init_state = (jnp.full((n_heads,), -jnp.inf, jnp.float32), jnp.zeros((n_heads,), jnp.float32), jnp.zeros((n_heads, head_dim), jnp.float32))
    n_blocks = row_len // block_len + 1
    run_max, run_sum, ctx_acc = lax.fori_loop(0, n_blocks, block_step, init_state)
    return (ctx_acc / run_sum[:, None]).astype(jnp.bfloat16)


def update_cache(cache_rows, new_rows, row_lens):
    positions = lax.broadcasted_iota(jnp.int32, (1, cache_rows.shape[1], 1), 1)
    return jnp.where(positions == row_lens[:, None, None], new_rows[:, None, :], cache_rows)


def solution(mesh):
    def group_step(hidden, w_query, w_key, w_value, w_out, key_cache, value_cache, lengths):
        n_rows = hidden.shape[0]
        local_rows = key_cache.shape[0]
        head_dim = key_cache.shape[2]
        local_heads = w_query.shape[1] // head_dim
        row_start = lax.axis_index('model') * local_rows
        query = jnp.dot(hidden, w_query, preferred_element_type=jnp.float32).astype(jnp.bfloat16)
        query = query.reshape(n_rows, local_heads, head_dim)
        query_local = lax.all_to_all(query, 'model', 0, 1, tiled=True)
        hidden_local = lax.dynamic_slice_in_dim(hidden, row_start, local_rows, 0)
        len_local = lax.dynamic_slice_in_dim(lengths, row_start, local_rows, 0)
        key_new = jnp.dot(hidden_local, w_key, preferred_element_type=jnp.float32).astype(jnp.bfloat16)
        value_new = jnp.dot(hidden_local, w_value, preferred_element_type=jnp.float32).astype(jnp.bfloat16)
        key_upd = update_cache(key_cache, key_new, len_local)
        value_upd = update_cache(value_cache, value_new, len_local)
        context = lax.map(attend_row, (query_local, key_upd, value_upd, len_local))
        context_back = lax.all_to_all(context, 'model', 1, 0, tiled=True)
        part_sum = jnp.dot(context_back.reshape(n_rows, local_heads * head_dim), w_out, preferred_element_type=jnp.float32).astype(jnp.bfloat16)
        attn_out = lax.psum(part_sum, 'model')
        hidden_out = (hidden.astype(jnp.float32) + attn_out.astype(jnp.float32)).astype(jnp.bfloat16)
        return hidden_out, key_upd, value_upd

    row_spec = P('replica', None)
    cache_spec = P(('replica', 'model'), None, None)
    return jax.shard_map(group_step, mesh=mesh, in_specs=(row_spec, P(None, 'model'), P(None, None), P(None, None), P('model', None), cache_spec, cache_spec, P('replica')), out_specs=(row_spec, cache_spec, cache_spec), check_vma=False)
```

profile of v0, /device:TPU:97, one launch (start us, length us, event | category | flops | bytes accessed | tf_op | source)
XLA Modules:
  0.0 841.6 jit_solution(12650380860019230303)
XLA Ops:
  7.2 15.8 %convolution_convert_fusion.1 = bf16[2048,256]{0,1:T(8,128)(2,1)S(1)} fusion(bf16[2048,8192]{1,0:T(8,128)(2,1)} %param.12, bf16[8192,256]{1,0:T(8,128)(2,1)} %param.13), kind=kOutput, calls=%fused_computation.28 | convolution fusion | flops 8590458880 | bytes 38797312 | tf_op jit(solution)/shard_map/dot_general | solution.py:48
  23.0 2.0 copy.18
  25.0 9.1 %all-to-all-start = ((bf16[2048,2,128]{2,1,0:T(2,128)(2,1)}), bf16[2048,2,128]{2,1,0:T(2,128)(2,1)S(1)}, u32[]{:S(2)}, u32[]{:S(2)}) async-start(bf16[2048,2,128]{2,1,0:T(2,128)(2,1)} %copy.18), calls=%async_computation | async-start | bytes 2097152 | tf_op jit(solution)/shard_map/all_to_all | solution.py:50
  35.0 1.7 convolution_convert_fusion.2
  36.7 2.4 convolution_convert_fusion.3
  39.2 11.9 %broadcast_select_fusion = (bf16[64,512,128]{2,1,0:T(8,128)(2,1)}, bf16[64,512,128]{2,1,0:T(8,128)(2,1)}) fusion(bf16[64,512,128]{2,1,0:T(8,128)(2,1)} %param.17, pred[64,512]{1,0:T(8,128)(4,1)S(1)} %iota_compare_fusion, bf16[64,128]{1,0:T(8,128)(2,1)S(1)} %convolution_convert_fusion.2, bf16[64,512,128]{2,1,0:T(8,128)(2,1)} %param.18, ...), kind=kLoop, calls=%fused_computation.26 | loop fusion | flops 8388608 | bytes 33619968 | tf_op jit(solution)/shard_map/jit(_where)/select_n | solution.py:38
  52.0 458.9 %while.39 = (s32[]{:T(128)}, bf16[64,64,128]{2,1,0:T(8,128)(2,1)}, s32[64]{0:T(128)S(1)}, bf16[64,512,128]{2,1,0:T(8,128)(2,1)}, bf16[64,64,128]{2,1,0:T(8,128)(...) while((s32[]{:T(128)}, bf16[64,64,128]{2,1,0:T(8,128)(2,1)}, ...), condition=%wide.region_5.6_spmd, body=%wide.region_0.5_spmd.sunk | while | flops 17171604 | bytes 1220904 | solution.py:57
  64.5 1.2 while.40
  78.8 1.2 while.40
  93.1 1.2 while.40
  107.5 1.2 while.40
  121.8 1.2 while.40
  136.2 1.2 while.40
  150.5 1.2 while.40
  164.8 1.2 while.40
  179.2 1.2 while.40
  193.5 1.2 while.40
  207.9 1.2 while.40
  222.2 1.2 while.40
  236.5 1.2 while.40
  265.2 1.2 while.40
  293.9 1.2 while.40
  336.9 1.2 while.40
  380.0 1.2 while.40
  408.6 1.2 while.40
  451.7 1.2 while.40
  494.7 1.2 while.40
  511.0 1.9 copy.22
  512.9 22.8 %all_to_all.33 = bf16[64,64,128]{2,0,1:T(8,128)(2,1)S(1)} all-to-all(bf16[64,64,128]{2,0,1:T(8,128)(2,1)S(1)} %copy.22), channel_id=1, replica_groups=mesh['replica'=1,'model'=32] {'model'}, dimensions={1} | all-to-all | bytes 2097152 | tf_op jit(solution)/shard_map/all_to_all | solution.py:58
  536.7 17.0 %convolution_convert_fusion = bf16[2048,8192]{1,0:T(8,128)(2,1)} fusion(bf16[256,8192]{1,0:T(8,128)(2,1)} %param.16, bf16[256,8,2,128]{3,2,1,0:T(2,128)(2,1)S(1)} %bitcast.41), kind=kOutput, calls=%fused_computation.25 | convolution fusion | flops 8606711808 | bytes 38797312 | tf_op jit(solution)/shard_map/dot_general | solution.py:59
  553.8 248.0 %all-reduce.2.cloned.1.call-done = bf16[2048,8192]{1,0:T(8,128)(2,1)} async-done(((bf16[2048,8192]{1,0:T(8,128)(2,1)}), bf16[2048,8192]{1,0:T(8,128)(2,1)}) %all-reduce.2.cloned.1.call-update) | async-done | bytes 33554448 | tf_op jit(solution)/shard_map/psum | solution.py:60
  801.9 32.8 %add_convert_fusion = bf16[2048,8192]{1,0:T(8,128)(2,1)} fusion(bf16[2048,8192]{1,0:T(8,128)(2,1)} %all-reduce.2.cloned.1.call-done, bf16[2048,8192]{1,0:T(8,128)(2,1)} %param.12), kind=kLoop, calls=%fused_computation.24 | loop fusion | flops 67108864 | bytes 100663296 | tf_op jit(solution)/shard_map/convert_element_type | solution.py:61
  (954 shorter events, 348.2 us)
Async XLA Ops:
  7.2 27.8 %copy-start = (bf16[8192,128]{1,0:T(8,128)(2,1)S(1)}, bf16[8192,128]{1,0:T(8,128)(2,1)}, u32[]{:S(2)}) copy-start(bf16[8192,128]{1,0:T(8,128)(2,1)} %param.14) | copy-start | bytes 6291460
  25.0 26.1 %all-to-all-start = ((bf16[2048,2,128]{2,1,0:T(2,128)(2,1)}), bf16[2048,2,128]{2,1,0:T(2,128)(2,1)S(1)}, u32[]{:S(2)}, u32[]{:S(2)}) async-start(bf16[2048,2,128]{2,1,0:T(2,128)(2,1)} %copy.18), calls=%async_computation | async-start | bytes 2097152 | tf_op jit(solution)/shard_map/all_to_all | solution.py:50
  34.1 767.7 %all-reduce.2.cloned.1.call-start = ((), (), s32[]{:S(2)}) async-start(), calls=%async_computation.2 | async-start | bytes 67108864 | tf_op jit(solution)/shard_map/psum | solution.py:60
  801.9 32.8 %copy-start.1 = (bf16[8192,128]{1,0:T(8,128)(2,1)S(1)}, bf16[8192,128]{1,0:T(8,128)(2,1)}, u32[]{:S(2)}) copy-start(bf16[8192,128]{1,0:T(8,128)(2,1)} %param.14) | copy-start | bytes 6291460
Sparse Core Ops, SparseCore 0:
  554.0 247.8 all-reduce.1
where the time goes:
time: 847 us; the launch traced here: 842 us
  waiting for transfers between devices  248 us (29%)
  loops' own time  168 us (20%)
  other arithmetic  151 us (18%)
  matrix products  120 us (14%)
  local copies, waits for them, and re-layouts  108 us (13%)
  blocking collectives  22.8 us (3%)
  between operations  14.2 us (2%)
  starting transfers between devices  9.2 us (1%)
    psum x1, waiting for transfers between devices, group_step(): attn_out = lax.psum(part_sum, 'model')  248 us
    another operation x1, loops' own time, group_step(): context = lax.map(attend_row, (query_local, key_upd, value_upd, len_local))  166 us
    dot_general x64, matrix products, block_step(): jnp.einsum('hd,td->ht', query_row, key_block, preferred_element_type=jnp....  68.5 us
    squeeze x64, local copies, waits for them, and re-layouts, group_step(): context = lax.map(attend_row, (query_local, key_upd, value_upd, len_local))  59.1 us
    dynamic_update_slice x64, other arithmetic, group_step(): context = lax.map(attend_row, (query_local, key_upd, value_upd, len_local))  44.5 us
    dynamic_slice x64, local copies, waits for them, and re-layouts, group_step(): context = lax.map(attend_row, (query_local, key_upd, value_upd, len_local))  41.3 us
    le x64, other arithmetic, block_step(): scores = jnp.where(positions <= row_len, scores, -jnp.inf)  40.8 us
    convert_element_type x1, other arithmetic, group_step(): (hidden.astype(jnp.float32) + attn_out.astype(jnp.float32)).astype(jnp.bf...  32.8 us
  transfers between devices with their start and end apart: 2, of which 1 were waited for; matrix products, arithmetic and copies ran while one was open for 2% of the time, Pallas kernels for 0%

commit v1 on v0

v1 whole, which is shorter than its diff:
```python
import functools
import math
import jax
import jax.numpy as jnp
from jax import lax
from jax.experimental import pallas as pl
from jax.experimental.pallas import tpu as pltpu
from jax.sharding import PartitionSpec as P

ROWS_PER_STEP = 4


def attend_kernel(len_ref, q_ref, kn_ref, vn_ref, k_ref, v_ref, ko_ref, vo_ref, ctx_ref):
    rows, seq_len, head_dim = k_ref.shape
    n_heads = q_ref.shape[1]
    scale = head_dim ** -0.5
    step = pl.program_id(0)
    tile = math.gcd(seq_len, 16)
    ko_ref[...] = k_ref[...]
    vo_ref[...] = v_ref[...]
    spans = [s for s in (128, 256) if s < seq_len] + [seq_len]
    for r in range(rows):
        row_len = len_ref[step * rows + r]
        base = pl.multiple_of((row_len // tile) * tile, tile)
        pick = lax.broadcasted_iota(jnp.int32, (tile, head_dim), 0) == row_len - base
        for new_ref, out_ref in ((kn_ref, ko_ref), (vn_ref, vo_ref)):
            new = jnp.broadcast_to(new_ref[0, r:r + 1, :], (tile, head_dim)).astype(jnp.float32)
            old = out_ref[r, pl.ds(base, tile), :].astype(jnp.float32)
            out_ref[r, pl.ds(base, tile), :] = jnp.where(pick, new, old).astype(jnp.bfloat16)
        lower = 0
        for span in spans:
            @pl.when((row_len >= lower) & (row_len < span))
            def _(span=span):
                s = lax.dot_general(q_ref[r], ko_ref[r, :span, :], (((1,), (1,)), ((), ())), preferred_element_type=jnp.float32) * scale
                pos = lax.broadcasted_iota(jnp.int32, (n_heads, span), 1)
                s = jnp.where(pos <= row_len, s, -jnp.inf)
                e = jnp.exp(s - jnp.max(s, axis=1, keepdims=True))
                total = jnp.sum(e, axis=1, keepdims=True)
                acc = jnp.dot(e.astype(jnp.bfloat16), vo_ref[r, :span, :], preferred_element_type=jnp.float32)
                ctx_ref[r] = (acc / total).astype(jnp.bfloat16)
            lower = span


def attend(lens, query, key_new, value_new, key_cache, value_cache):
    n, seq_len, head_dim = key_cache.shape
    n_heads = query.shape[1]
    rows = math.gcd(n, ROWS_PER_STEP)
    cache = pl.BlockSpec((rows, seq_len, head_dim), lambda i, lens: (i, 0, 0))
    new = pl.BlockSpec((1, rows, head_dim), lambda i, lens: (i, 0, 0))
    heads = pl.BlockSpec((rows, n_heads, head_dim), lambda i, lens: (i, 0, 0))
    return pl.pallas_call(
        attend_kernel,
        grid_spec=pltpu.PrefetchScalarGridSpec(
            num_scalar_prefetch=1,
            grid=(n // rows,),
            in_specs=[heads, new, new, cache, cache],
            out_specs=[cache, cache, heads],
        ),
        out_shape=[
            jax.ShapeDtypeStruct(key_cache.shape, key_cache.dtype),
            jax.ShapeDtypeStruct(value_cache.shape, value_cache.dtype),
            jax.ShapeDtypeStruct(query.shape, jnp.bfloat16),
        ],
        cost_estimate=pl.CostEstimate(flops=4 * n * n_heads * seq_len * head_dim, bytes_accessed=8 * n * seq_len * head_dim, transcendentals=0),
        name='attend',
    )(lens, query, key_new.reshape(n // rows, rows, head_dim), value_new.reshape(n // rows, rows, head_dim), key_cache, value_cache)


def solution(mesh):
    def group_step(hidden, w_query, w_key, w_value, w_out, key_cache, value_cache, lengths):
        n_rows = hidden.shape[0]
        local_rows = key_cache.shape[0]
        head_dim = key_cache.shape[2]
        local_heads = w_query.shape[1] // head_dim
        row_start = lax.axis_index('model') * local_rows
        query = jnp.dot(hidden, w_query, preferred_element_type=jnp.float32).astype(jnp.bfloat16)
        query = query.reshape(n_rows, local_heads, head_dim)
        query_local = lax.all_to_all(query, 'model', 0, 1, tiled=True)
        hidden_local = lax.dynamic_slice_in_dim(hidden, row_start, local_rows, 0)
        len_local = lax.dynamic_slice_in_dim(lengths, row_start, local_rows, 0)
        key_new = jnp.dot(hidden_local, w_key, preferred_element_type=jnp.float32).astype(jnp.bfloat16)
        value_new = jnp.dot(hidden_local, w_value, preferred_element_type=jnp.float32).astype(jnp.bfloat16)
        key_upd, value_upd, context = attend(len_local, query_local, key_new, value_new, key_cache, value_cache)
        context_back = lax.all_to_all(context, 'model', 1, 0, tiled=True)
        part_sum = jnp.dot(context_back.reshape(n_rows, local_heads * head_dim), w_out, preferred_element_type=jnp.float32).astype(jnp.bfloat16)
        attn_out = lax.psum(part_sum, 'model')
        hidden_out = (hidden.astype(jnp.float32) + attn_out.astype(jnp.float32)).astype(jnp.bfloat16)
        return hidden_out, key_upd, value_upd

    row_spec = P('replica', None)
    cache_spec = P(('replica', 'model'), None, None)
    return jax.shard_map(group_step, mesh=mesh, in_specs=(row_spec, P(None, 'model'), P(None, None), P(None, None), P('model', None), cache_spec, cache_spec, P('replica')), out_specs=(row_spec, cache_spec, cache_spec), check_vma=False)
```

time: 847 us -> 411 us (0.49)
  loops' own time: 168 us -> 0 us
  other arithmetic: 151 us -> 32.8 us
  local copies, waits for them, and re-layouts: 108 us -> 8.52 us
  matrix products: 120 us -> 38.2 us
  Pallas kernels: 0 us -> 28.8 us
  waiting for transfers between devices: 248 us -> 258 us
    another operation x65 -> x0, loops' own time: 168 us -> none  [the longest x1 166 us: group_step(): context = lax.map(attend_row, (query_local, key_upd, value_upd, len_local))]
    dot_general x128 -> x0, matrix products: 83.1 us -> none  [the longest x64 68.5 us: block_step(): jnp.einsum('hd,td->ht', query_row, key_block, preferred_element_type=jnp....]
    squeeze x64 -> x0, local copies, waits for them, and re-layouts: 59.1 us -> none  [group_step(): context = lax.map(attend_row, (query_local, key_upd, value_upd, len_local))]
    dynamic_update_slice x64 -> x0, other arithmetic: 44.5 us -> none  [group_step(): context = lax.map(attend_row, (query_local, key_upd, value_upd, len_local))]
    dynamic_slice x64 -> x0, local copies, waits for them, and re-layouts: 41.3 us -> none  [group_step(): context = lax.map(attend_row, (query_local, key_upd, value_upd, len_local))]
    le x64 -> x0, other arithmetic: 40.8 us -> none  [block_step(): scores = jnp.where(positions <= row_len, scores, -jnp.inf)]
    pallas_call x0 -> x1, Pallas kernels: none -> 28.8 us  [attend(): pl.pallas_call(attend_kernel, grid_spec=pltpu.PrefetchScalarGridSpec(num_...]
    reduce_sum x64 -> x0, other arithmetic: 12.5 us -> none  [block_step(): run_sum = rescale * run_sum + jnp.sum(weights, axis=1)]
  transfers between devices with their start and end apart: 2 -> 2, of which waited for: 1 -> 2; matrix products, arithmetic and copies ran while one was open for 2% -> 2% of each run, Pallas kernels for 0% -> 0%
where the time goes in v1:
time: 411 us; the launch traced here: 410 us
  waiting for transfers between devices  258 us (63%)
  matrix products  38.2 us (9%)
  other arithmetic  32.8 us (8%)
  Pallas kernels  28.8 us (7%)
  blocking collectives  20.1 us (5%)
  between operations  14.1 us (3%)
  starting transfers between devices  9.2 us (2%)
  local copies, waits for them, and re-layouts  8.52 us (2%)
    psum x1, waiting for transfers between devices, group_step(): attn_out = lax.psum(part_sum, 'model')  248 us
    convert_element_type x1, other arithmetic, group_step(): (hidden.astype(jnp.float32) + attn_out.astype(jnp.float32)).astype(jnp.bf...  32.8 us
    pallas_call x1, Pallas kernels, attend(): pl.pallas_call(attend_kernel, grid_spec=pltpu.PrefetchScalarGridSpec(num_...  28.8 us
    all_to_all x1, blocking collectives, group_step(): context_back = lax.all_to_all(context, 'model', 1, 0, tiled=True)  20.1 us
    dot_general x1, matrix products, group_step(): jnp.dot(context_back.reshape(n_rows, local_heads * head_dim), w_out, pref...  17 us
    dot_general x1, matrix products, group_step(): jnp.dot(hidden, w_query, preferred_element_type=jnp.float32)  15.8 us
    all_to_all x1, waiting for transfers between devices, group_step(): query_local = lax.all_to_all(query, 'model', 0, 1, tiled=True)  9.81 us
    all_to_all x1, starting transfers between devices, group_step(): query_local = lax.all_to_all(query, 'model', 0, 1, tiled=True)  9.14 us
  transfers between devices with their start and end apart: 2, of which 2 were waited for; matrix products, arithmetic and copies ran while one was open for 2% of the time, Pallas kernels for 0%

profile of v1, /device:TPU:97, one launch (start us, length us, event | category | flops | bytes accessed | tf_op | source)
XLA Modules:
  0.0 409.6 jit_solution(2606184204302209086)
XLA Ops:
  7.2 0.0 copy-start
  7.2 15.8 %convolution_convert_fusion.1 = bf16[2048,256]{0,1:T(8,128)(2,1)S(1)} fusion(bf16[2048,8192]{1,0:T(8,128)(2,1)} %param.8, bf16[8192,256]{1,0:T(8,128)(2,1)} %param.9), kind=kOutput, calls=%fused_computation.2 | convolution fusion | flops 8590458880 | bytes 38797312 | tf_op jit(solution)/shard_map/dot_general | solution.py:76
  23.0 2.0 copy.14
  25.0 9.1 %all-to-all-start = ((bf16[2048,2,128]{2,1,0:T(2,128)(2,1)}), bf16[2048,2,128]{2,1,0:T(2,128)(2,1)S(1)}, u32[]{:S(2)}, u32[]{:S(2)}) async-start(bf16[2048,2,128]{2,1,0:T(2,128)(2,1)} %copy.14), calls=%async_computation | async-start | bytes 2097152 | tf_op jit(solution)/shard_map/all_to_all | solution.py:78
  34.1 0.1 all-reduce.2.cloned.1.call-start
  34.2 1.3 dynamic_slice.6.len_ref
  35.6 0.0 copy-done
  35.6 2.3 convolution_convert_fusion.3
  37.9 3.0 convolution_convert_fusion.2
  40.9 9.8 %all-to-all-done = bf16[2048,2,128]{2,1,0:T(2,128)(2,1)S(1)} async-done(((bf16[2048,2,128]{2,1,0:T(2,128)(2,1)}), bf16[2048,2,128]{2,1,0:T(2,128)(2,1)S(1)}, u32[]{:S(2)}, u32[]{:S(2)}) %all-to-all-start) | async-done | bytes 1048608 | tf_op jit(solution)/shard_map/all_to_all | solution.py:78
  50.7 0.1 copy.15
  50.8 2.1 copy.16
  52.9 28.8 %attend.1 = (bf16[64,512,128]{2,1,0:T(8,128)(2,1)}, bf16[64,512,128]{2,1,0:T(8,128)(2,1)}, bf16[64,64,128]{2,1,0:T(8,128)(2,1)}) custom-call(s32[64]{0:T(128)} %dynamic_slice.6.len_ref, bf16[64,64,128]{2,1,0:T(8,128)(2,1)} %bitcast.20, bf16[16,4,128]{2,1,0:T(4,128)(2,1)} %bitcast.24, bf16[16,4,128]{2,1,0:T(4,128)(2,1)} %bitcast.25, ...), custom_call_target="tpu_custom_call" | custom-call | flops 1073741824 | bytes 33554432 | tf_op jit(solution)/shard_map/attend/pallas_call | solution.py:51
  81.7 1.9 copy.17
  83.6 20.1 %all_to_all.33 = bf16[64,64,128]{2,0,1:T(8,128)(2,1)S(1)} all-to-all(bf16[64,64,128]{2,0,1:T(8,128)(2,1)S(1)} %copy.17), channel_id=1, replica_groups=mesh['replica'=1,'model'=32] {'model'}, dimensions={1} | all-to-all | bytes 2097152 | tf_op jit(solution)/shard_map/all_to_all | solution.py:84
  103.7 1.1 copy.18
  104.8 17.0 %convolution_convert_fusion = bf16[2048,8192]{1,0:T(8,128)(2,1)} fusion(bf16[256,8192]{1,0:T(8,128)(2,1)} %param.12, bf16[256,8,2,128]{3,2,1,0:T(2,128)(2,1)S(1)} %bitcast.19), kind=kOutput, calls=%fused_computation.1 | convolution fusion | flops 8606711808 | bytes 38797312 | tf_op jit(solution)/shard_map/dot_general | solution.py:85
  121.8 0.1 all-reduce.2.cloned.1.call-update
  121.9 248.0 %all-reduce.2.cloned.1.call-done = bf16[2048,8192]{1,0:T(8,128)(2,1)} async-done(((bf16[2048,8192]{1,0:T(8,128)(2,1)}), bf16[2048,8192]{1,0:T(8,128)(2,1)}) %all-reduce.2.cloned.1.call-update) | async-done | bytes 33554448 | tf_op jit(solution)/shard_map/psum | solution.py:86
  369.9 0.0 copy-start.1
  369.9 32.8 %add_convert_fusion = bf16[2048,8192]{1,0:T(8,128)(2,1)} fusion(bf16[2048,8192]{1,0:T(8,128)(2,1)} %all-reduce.2.cloned.1.call-done, bf16[2048,8192]{1,0:T(8,128)(2,1)} %param.8), kind=kLoop, calls=%fused_computation | loop fusion | flops 67108864 | bytes 100663296 | tf_op jit(solution)/shard_map/convert_element_type | solution.py:87
  402.7 0.0 copy-done.1
Async XLA Ops:
  7.2 28.4 %copy-start = (bf16[8192,128]{1,0:T(8,128)(2,1)S(1)}, bf16[8192,128]{1,0:T(8,128)(2,1)}, u32[]{:S(2)}) copy-start(bf16[8192,128]{1,0:T(8,128)(2,1)} %param.10) | copy-start | bytes 6291460
  25.0 25.7 %all-to-all-start = ((bf16[2048,2,128]{2,1,0:T(2,128)(2,1)}), bf16[2048,2,128]{2,1,0:T(2,128)(2,1)S(1)}, u32[]{:S(2)}, u32[]{:S(2)}) async-start(bf16[2048,2,128]{2,1,0:T(2,128)(2,1)} %copy.14), calls=%async_computation | async-start | bytes 2097152 | tf_op jit(solution)/shard_map/all_to_all | solution.py:78
  34.1 335.8 %all-reduce.2.cloned.1.call-start = ((), (), s32[]{:S(2)}) async-start(), calls=%async_computation.2 | async-start | bytes 67108864 | tf_op jit(solution)/shard_map/psum | solution.py:86
  369.9 32.8 %copy-start.1 = (bf16[8192,128]{1,0:T(8,128)(2,1)S(1)}, bf16[8192,128]{1,0:T(8,128)(2,1)}, u32[]{:S(2)}) copy-start(bf16[8192,128]{1,0:T(8,128)(2,1)} %param.10) | copy-start | bytes 6291460
Sparse Core Ops, SparseCore 0:
  122.0 247.8 all-reduce.1

commit v2 on v1

--- a/solution.py
+++ b/solution.py
@@ -66,26 +66,364 @@
     )(lens, query, key_new.reshape(n // rows, rows, head_dim), value_new.reshape(n // rows, rows, head_dim), key_cache, value_cache)
 
 
+MESH = pl.DeviceIdType.MESH
+CORES = 2
+
+
+class Moves:
+    def __init__(self, send_sems, recv_sems):
+        self.send_sems, self.recv_sems = send_sems, recv_sems
+        self.count, self.copies, self.unsent = 0, {}, []
+
+    def send(self, key, src, dst, device):
+        copy = pltpu.make_async_remote_copy(src_ref=src, dst_ref=dst, send_sem=self.send_sems.at[self.count], recv_sem=self.recv_sems.at[self.count], device_id={'model': device}, device_id_type=MESH)
+        copy.start()
+        self.count += 1
+        self.copies[key] = copy
+        self.unsent.append(copy)
+
+    def local(self, key, src, dst):
+        copy = pltpu.make_async_copy(src, dst, self.send_sems.at[self.count])
+        copy.start()
+        self.count += 1
+        self.copies[key] = copy
+
+    def got(self, key):
+        self.copies.pop(key).wait_recv()
+
+    def done(self, key):
+        self.copies.pop(key).wait()
+
+    def finish(self):
+        for copy in self.unsent:
+            copy.wait_send()
+
+
+def place(side):
+    me = lax.axis_index('model')
+    return me // (CORES * side), lax.rem(me // CORES, side), lax.rem(me, CORES)
+
+
+def greet(devices):
+    barrier = pltpu.get_barrier_semaphore()
+    for device in devices:
+        pl.semaphore_signal(barrier, inc=1, device_id={'model': device}, device_id_type=MESH)
+    pl.semaphore_wait(barrier, len(devices))
+
+
+def columns(start, width):
+    return pl.ds(pl.multiple_of(start * width, width), width)
+
+
+def query_kernel(side, hid_ref, wq_ref, wo_ref, q_ref, wa_ref, wb_ref, wq_all, hid, q_buf, acc, relay, own_w, send_sems, recv_sems):
+    y, x, c = place(side)
+    rows, dim = hid_ref.shape[3:]
+    half = wq_ref.shape[1]
+    w_rows = wo_ref.shape[0]
+    width = wo_ref.shape[1] // (2 * side)
+    w_refs = (wa_ref, wb_ref)
+    step = lambda a, d: lax.rem(a + d + side, side)
+    dev = lambda yy, xx: (yy * side + xx) * CORES + c
+    other = (y * side + x) * CORES + 1 - c
+    peers = [(dy, dx) for dy in range(side) for dx in range(side) if dy or dx]
+    greet([dev(step(y, dy), step(x, dx)) for dy, dx in peers] + [other])
+    mv = Moves(send_sems, recv_sems)
+    order = list(range(1, side)) + [0]
+    mv.send('wq', wq_ref, wq_all.at[c], other)
+    mv.local('wq_own', wq_ref, wq_all.at[c])
+    for i, dy in enumerate(order):
+        mv.local(('hid', i), hid_ref.at[step(y, dy), :, c], hid.at[i])
+    along = ((x, lambda u: dev(y, u)), (y, lambda u: dev(u, x)))
+    wcols = lambda t, u: columns(t * side + u, width)
+    top, low = pl.ds(0, w_rows // 2), pl.ds(w_rows // 2, w_rows // 2)
+    for t, (u, at) in enumerate(along):
+        mv.send(('w1R', t), wo_ref.at[top, wcols(t, step(u, 2))], relay.at[t, 0], at(step(u, 1)))
+        mv.send(('w1L', t), wo_ref.at[low, wcols(t, step(u, 2))], relay.at[t, 1], at(step(u, -1)))
+        mv.local(('w_own', t), wo_ref.at[:, wcols(t, u)], own_w.at[t])
+    for t, (u, at) in enumerate(along):
+        mv.send(('wR', t), wo_ref.at[:, wcols(t, step(u, 1))], w_refs[t].at[u, c], at(step(u, 1)))
+        mv.send(('wL', t), wo_ref.at[:, wcols(t, step(u, -1))], w_refs[t].at[u, c], at(step(u, -1)))
+        mv.send(('wS', t, 0), wo_ref.at[:, wcols(t, u)], w_refs[t].at[u, c], other)
+
+    depth = min(1024, dim)
+
+    def project(i, core):
+        acc[...] = jnp.zeros_like(acc)
+
+        @pl.loop(0, dim // depth)
+        def _(k):
+            part = columns(k, depth)
+            acc[...] += jnp.dot(hid[i, :, :, part].reshape(side * rows, depth), wq_all[core, part, :], preferred_element_type=jnp.float32)
+
+        q_buf[i, :, :, columns(core, half)] = acc[...].astype(jnp.bfloat16).reshape(side, rows, half)
+
+    mv.done('wq_own')
+    for i in range(side):
+        mv.done(('hid', i))
+        project(i, c)
+    for t, (u, at) in enumerate(along):
+        mv.done(('w_own', t))
+        mv.local(('w_put', t), own_w.at[t], w_refs[t].at[u, c])
+        mv.got(('w1R', t))
+        mv.send(('w2R', t), relay.at[t, 0], w_refs[t].at[step(u, -1), c, top], at(step(u, 1)))
+        mv.got(('w1L', t))
+        mv.send(('w2L', t), relay.at[t, 1], w_refs[t].at[step(u, 1), c, low], at(step(u, -1)))
+    mv.got('wq')
+    for i, dy in enumerate(order):
+        project(i, 1 - c)
+        for dx in [d for d in (2, 1, 3, 0)][:side]:
+            if dy or dx:
+                mv.send(('q', dy, dx), q_buf.at[i, step(x, dx)], q_ref.at[y, x], dev(step(y, dy), step(x, dx)))
+            else:
+                mv.local('q_own', q_buf.at[i, x], q_ref.at[y, x])
+    for t, (u, at) in enumerate(along):
+        mv.got(('wR', t))
+        mv.send(('wS', t, 1), w_refs[t].at[step(u, -1), c], w_refs[t].at[step(u, -1), c], other)
+        mv.got(('wL', t))
+        mv.send(('wS', t, 3), w_refs[t].at[step(u, 1), c], w_refs[t].at[step(u, 1), c], other)
+    for t, (u, at) in enumerate(along):
+        mv.got(('w2R', t))
+        mv.got(('w2L', t))
+        mv.send(('wS', t, 2), w_refs[t].at[step(u, 2), c], w_refs[t].at[step(u, 2), c], other)
+    for dy, dx in peers:
+        mv.got(('q', dy, dx))
+    mv.done('q_own')
+    for t in range(2):
+        mv.done(('w_put', t))
+        for d in range(side):
+            mv.got(('wS', t, d))
+    mv.finish()
+
+
+def output_kernel(side, ctx_ref, wa_ref, wb_ref, hid_ref, out_ref, held, w_buf, hid, acc, part, first, second, final, send_sems, recv_sems):
+    y, x, c = place(side)
+    rows, depth = ctx_ref.shape[2:]
+    width = w_buf.shape[-1]
+    step = lambda a, d: lax.rem(a + d + side, side)
+    dev = lambda yy, xx: (yy * side + xx) * CORES + c
+    other = (y * side + x) * CORES + 1 - c
+    spots = ((y, x), (x, y))
+    at = lambda t, v, u: dev(v, u) if t == 0 else dev(u, v)
+    ctx_of = lambda t, v: ctx_ref.at[v] if t == 0 else ctx_ref.at[:, v]
+    greet([dev(y, step(x, d)) for d in range(1, side)] + [dev(step(y, d), x) for d in range(1, side)] + [other])
+    mv = Moves(send_sems, recv_sems)
+    both = range(2)
+
+    def view(ref, t, v, g, us=None):
+        us = slice(None) if us is None else us
+        cols = columns(t * side + g, width)
+        return ref.at[v, us, c, :, cols] if t == 0 else ref.at[us, v, c, :, cols]
+
+    for t in both:
+        v, u = spots[t]
+        mv.send(('a', t, 2), ctx_of(t, step(v, 2)), held.at[t, u, v], at(t, step(v, 2), u))
+    for t in both:
+        v, u = spots[t]
+        for d in (1, 3):
+            mv.send(('a', t, d), ctx_of(t, step(v, d)), held.at[t, u, v], at(t, step(v, d), u))
+        mv.send(('gR', t, 0), ctx_of(t, v), held.at[t, u, v], at(t, v, step(u, 1)))
+        mv.send(('gL', t, 0), ctx_of(t, v), held.at[t, u, v], at(t, v, step(u, -1)))
+    for t in both:
+        v, u = spots[t]
+        mv.local(('w', t), (wa_ref, wb_ref)[t], w_buf.at[t])
+        mv.local(('hid', t), view(hid_ref, t, v, u), hid.at[t])
+    for p in (1, 3, 2):
+        for t in both:
+            v, u = spots[t]
+            mv.got(('a', t, p))
+            slot = held.at[t, u, step(v, -p)]
+            mv.send(('gR', t, p), slot, slot, at(t, v, step(u, 1)))
+            mv.send(('gL', t, p), slot, slot, at(t, v, step(u, -1)))
+    for p in (0, 1, 3, 2):
+        for t in both:
+            v, u = spots[t]
+            mv.got(('gR', t, p))
+            if p in (0, 2):
+                slot = held.at[t, step(u, -1), step(v, -p)]
+                mv.send(('f', t, p), slot, slot, at(t, v, step(u, 1)))
+            mv.got(('gL', t, p))
+            if p in (1, 3):
+                slot = held.at[t, step(u, 1), step(v, -p)]
+                mv.send(('f', t, p), slot, slot, at(t, v, step(u, -1)))
+    for t in both:
+        mv.done(('w', t))
+
+    def product(t, p):
+        v, u = spots[t]
+        total = None
+        for k in range(side):
+            pieces = []
+            for d in range(side):
+                if p == 0 and d == 0:
+                    pieces.append(ctx_ref[v, k] if t == 0 else ctx_ref[k, v])
+                else:
+                    pieces.append(held[t, step(u, d), step(v, -p), k])
+            one = jnp.dot(jnp.concatenate(pieces, axis=0), w_buf[t, k].reshape(depth, width), preferred_element_type=jnp.float32)
+            total = one if total is None else total + one
+        acc[t] = total.reshape(side, rows, width)
+
+    upper, lower = pl.ds(0, side // 2), pl.ds(side // 2, side // 2)
+    for t in both:
+        v, u = spots[t]
+        mv.got(('f', t, 2))
+        product(t, 2)
+        part[t, 2] = acc[t].astype(jnp.bfloat16)
+        mv.send(('r1R', t), part.at[t, 2, upper], first.at[t, 0], at(t, step(v, 1), u))
+        mv.send(('r1L', t), part.at[t, 2, lower], first.at[t, 1], at(t, step(v, -1), u))
+    for p, now, later, tag, d in ((1, upper, lower, 'L', 1), (3, lower, upper, 'R', 0)):
+        for t in both:
+            v, u = spots[t]
+            to = at(t, step(v, -p), u)
+            mv.got(('f', t, p))
+            product(t, p)
+            part[t, p, now] = acc[t, now].astype(jnp.bfloat16)
+            mv.send(('r2' + tag, t), part.at[t, p, now], second.at[t, d, now], to)
+            mv.got(('r1' + tag, t))
+            part[t, p, later] = (acc[t, later] + first[t, d].astype(jnp.float32)).astype(jnp.bfloat16)
+            mv.send(('r3' + tag, t), part.at[t, p, later], second.at[t, d, later], to)
+    for t in both:
+        mv.got(('f', t, 0))
+        product(t, 0)
+    for t in both:
+        v, u = spots[t]
+        for tag in 'RL':
+            mv.got(('r2' + tag, t))
+            mv.got(('r3' + tag, t))
+        mv.done(('hid', t))
+        for d in range(side):
+            us = step(u, d)
+            y_sum = acc[t, d] + second[t, 0, d].astype(jnp.float32) + second[t, 1, d].astype(jnp.float32)
+            final[t, us] = (hid[t, us].astype(jnp.float32) + y_sum).astype(jnp.bfloat16)
+        mine = view(out_ref, t, v, u)
+        mv.send(('oR', t), final.at[t], mine, at(t, v, step(u, 1)))
+        mv.send(('oL', t), final.at[t], mine, at(t, v, step(u, -1)))
+        mv.send(('pR', t, 0), final.at[t], mine, at(t, step(v, 1), u))
+        mv.send(('pL', t, 0), final.at[t], mine, at(t, step(v, -1), u))
+        mv.local(('own', t), final.at[t], mine)
+        mv.send(('s', t, 0, 0), final.at[t], mine, other)
+    for t in both:
+        v, u = spots[t]
+        mv.got(('oR', t))
+        half = view(out_ref, t, v, step(u, -1), upper)
+        mv.send(('o2R', t), half, half, at(t, v, step(u, 1)))
+        mv.got(('oL', t))
+        half = view(out_ref, t, v, step(u, 1), lower)
+        mv.send(('o2L', t), half, half, at(t, v, step(u, -1)))
+    offsets = (0, -1, 1, 2)
+    for g in (1, 2, 3):
+        for t in both:
+            v, u = spots[t]
+            if g == 3:
+                mv.got(('o2R', t))
+                mv.got(('o2L', t))
+            piece = view(out_ref, t, v, step(u, offsets[g]))
+            mv.send(('pR', t, g), piece, piece, at(t, step(v, 1), u))
+            mv.send(('pL', t, g), piece, piece, at(t, step(v, -1), u))
+            mv.send(('s', t, 0, g), piece, piece, other)
+    for g in range(4):
+        for t in both:
+            v, u = spots[t]
+            mv.got(('pR', t, g))
+            piece = view(out_ref, t, step(v, -1), step(u, offsets[g]))
+            if g in (0, 2):
+                mv.send(('z', t, g), piece, piece, at(t, step(v, 1), u))
+            mv.send(('s', t, 1, g), piece, piece, other)
+            mv.got(('pL', t, g))
+            piece = view(out_ref, t, step(v, 1), step(u, offsets[g]))
+            if g in (1, 3):
+                mv.send(('z', t, g), piece, piece, at(t, step(v, -1), u))
+            mv.send(('s', t, 2, g), piece, piece, other)
+    for g in range(4):
+        for t in both:
+            v, u = spots[t]
+            mv.got(('z', t, g))
+            piece = view(out_ref, t, step(v, 2), step(u, offsets[g]))
+            mv.send(('s', t, 3, g), piece, piece, other)
+    for t in both:
+        mv.done(('own', t))
+        for i in range(4):
+            for g in range(4):
+                mv.got(('s', t, i, g))
+    mv.finish()
+
+
+ANY = pl.BlockSpec(memory_space=pl.ANY)
+VMEM = pl.BlockSpec(memory_space=pltpu.VMEM)
+
+
+def sems(n):
+    return [pltpu.SemaphoreType.DMA((n,)), pltpu.SemaphoreType.DMA((n,))]
+
+
+def project_queries(side, hidden, w_query, w_out):
+    rows, dim = hidden.shape[3:]
+    half = w_query.shape[1]
+    w_rows, width = w_out.shape[0], w_out.shape[1] // (2 * side)
+    bf16 = jnp.bfloat16
+    tile = jax.ShapeDtypeStruct((side, CORES, w_rows, width), bf16)
+    return pl.pallas_call(
+        functools.partial(query_kernel, side),
+        out_shape=[jax.ShapeDtypeStruct((side, side, rows, CORES * half), bf16), tile, tile],
+        in_specs=[ANY] * 3,
+        out_specs=[ANY] * 3,
+        scratch_shapes=[
+            pltpu.VMEM((CORES, dim, half), bf16),
+            pltpu.VMEM((side, side, rows, dim), bf16),
+            pltpu.VMEM((side, side, rows, CORES * half), bf16),
+            pltpu.VMEM((side * rows, half), jnp.float32),
+            pltpu.VMEM((2, 2, w_rows // 2, width), bf16),
+            pltpu.VMEM((2, w_rows, width), bf16),
+        ] + sems(64),
+        compiler_params=pltpu.CompilerParams(collective_id=0, has_side_effects=True, vmem_limit_bytes=60 << 20),
+        name='project_queries',
+    )(hidden, w_query, w_out)
+
+
+def project_context(side, context, w_a, w_b, hidden):
+    rows, depth = context.shape[2:]
+    width = w_a.shape[-1]
+    bf16, f32 = jnp.bfloat16, jnp.float32
+    return pl.pallas_call(
+        functools.partial(output_kernel, side),
+        out_shape=jax.ShapeDtypeStruct(hidden.shape, bf16),
+        in_specs=[VMEM, ANY, ANY, ANY],
+        out_specs=ANY,
+        scratch_shapes=[
+            pltpu.VMEM((2, side, side, side, rows, depth), bf16),
+            pltpu.VMEM((2,) + w_a.shape, bf16),
+            pltpu.VMEM((2, side, rows, width), bf16),
+            pltpu.VMEM((2, side, rows, width), f32),
+            pltpu.VMEM((2, 4, side, rows, width), bf16),
+            pltpu.VMEM((2, 2, side // 2, rows, width), bf16),
+            pltpu.VMEM((2, 2, side, rows, width), bf16),
+            pltpu.VMEM((2, side, rows, width), bf16),
+        ] + sems(128),
+        compiler_params=pltpu.CompilerParams(collective_id=1, has_side_effects=True, vmem_limit_bytes=60 << 20),
+        name='project_context',
+    )(context, w_a, w_b, hidden)
+
+
 def solution(mesh):
+    side = math.isqrt(mesh.shape['model'] // CORES)
+
     def group_step(hidden, w_query, w_key, w_value, w_out, key_cache, value_cache, lengths):
-        n_rows = hidden.shape[0]
+        n_rows, dim = hidden.shape
         local_rows = key_cache.shape[0]
         head_dim = key_cache.shape[2]
-        local_heads = w_query.shape[1] // head_dim
+        chip_cols = CORES * w_query.shape[1]
+        n_heads = side * side * chip_cols // head_dim
         row_start = lax.axis_index('model') * local_rows
-        query = jnp.dot(hidden, w_query, preferred_element_type=jnp.float32).astype(jnp.bfloat16)
-        query = query.reshape(n_rows, local_heads, head_dim)
-        query_local = lax.all_to_all(query, 'model', 0, 1, tiled=True)
+        hidden_tiles = hidden.reshape(side, side, CORES, local_rows, dim)
+        query, w_a, w_b = project_queries(side, hidden_tiles, w_query, w_out)
+        query = query.reshape(side * side, local_rows, chip_cols // head_dim, head_dim).transpose(1, 0, 2, 3).reshape(local_rows, n_heads, head_dim)
         hidden_local = lax.dynamic_slice_in_dim(hidden, row_start, local_rows, 0)
         len_local = lax.dynamic_slice_in_dim(lengths, row_start, local_rows, 0)
         key_new = jnp.dot(hidden_local, w_key, preferred_element_type=jnp.float32).astype(jnp.bfloat16)
         value_new = jnp.dot(hidden_local, w_value, preferred_element_type=jnp.float32).astype(jnp.bfloat16)
-        key_upd, value_upd, context = attend(len_local, query_local, key_new, value_new, key_cache, value_cache)
-        context_back = lax.all_to_all(context, 'model', 1, 0, tiled=True)
-        part_sum = jnp.dot(context_back.reshape(n_rows, local_heads * head_dim), w_out, preferred_element_type=jnp.float32).astype(jnp.bfloat16)
-        attn_out = lax.psum(part_sum, 'model')
-        hidden_out = (hidden.astype(jnp.float32) + attn_out.astype(jnp.float32)).astype(jnp.bfloat16)
-        return hidden_out, key_upd, value_upd
+        key_upd, value_upd, context = attend(len_local, query, key_new, value_new, key_cache, value_cache)
+        context = context.reshape(local_rows, side * side, chip_cols // head_dim, head_dim).transpose(1, 0, 2, 3).reshape(side, side, local_rows, chip_cols)
+        hidden_out = project_context(side, context, w_a, w_b, hidden_tiles)
+        return hidden_out.reshape(n_rows, dim), key_upd, value_upd
 
     row_spec = P('replica', None)
     cache_spec = P(('replica', 'model'), None, None)

time: 411 us -> 279 us (0.68)
  waiting for transfers between devices: 258 us -> 0 us
  Pallas kernels: 28.8 us -> 242 us
  matrix products: 38.2 us -> 5.33 us
  other arithmetic: 32.8 us -> 0 us
  local copies, waits for them, and re-layouts: 8.52 us -> 30.6 us
  blocking collectives: 20.1 us -> 0 us
  between operations: 14.1 us -> 0.84 us
  starting transfers between devices: 9.2 us -> 0 us
    psum x1 -> x0, waiting for transfers between devices: 248 us -> none  [group_step(): attn_out = lax.psum(part_sum, 'model')]
    pallas_call x0 -> x2, Pallas kernels: none -> 213 us  [the longest x1 167 us: project_context(): pl.pallas_call(functools.partial(output_kernel, side), out_shape=jax.Shap...]
    convert_element_type x1 -> x0, other arithmetic: 32.8 us -> none  [group_step(): (hidden.astype(jnp.float32) + attn_out.astype(jnp.float32)).astype(jnp.bf...]
    dot_general x2 -> x0, matrix products: 32.8 us -> none  [the longest x1 17 us: group_step(): jnp.dot(context_back.reshape(n_rows, local_heads * head_dim), w_out, pref...]
    unnamed x4 -> x5, local copies, waits for them, and re-layouts: 0.02 us -> 23.3 us
    all_to_all x1 -> x0, blocking collectives: 20.1 us -> none  [group_step(): context_back = lax.all_to_all(context, 'model', 1, 0, tiled=True)]
    all_to_all x1 -> x0, waiting for transfers between devices: 9.81 us -> none  [group_step(): query_local = lax.all_to_all(query, 'model', 0, 1, tiled=True)]
    all_to_all x1 -> x0, starting transfers between devices: 9.14 us -> none  [group_step(): query_local = lax.all_to_all(query, 'model', 0, 1, tiled=True)]
  transfers between devices with their start and end apart: 2 -> 0, of which waited for: 2 -> 0; matrix products, arithmetic and copies ran while one was open for 2% -> 0% of each run, Pallas kernels for 0% -> 0%
where the time goes in v2:
time: 279 us; the launch traced here: 278 us
  Pallas kernels  242 us (87%)
  local copies, waits for them, and re-layouts  30.6 us (11%)
  matrix products  5.33 us (2%)
    pallas_call x1, Pallas kernels, project_context(): pl.pallas_call(functools.partial(output_kernel, side), out_shape=jax.Shap...  167 us
    pallas_call x1, Pallas kernels, project_queries(): pl.pallas_call(functools.partial(query_kernel, side), out_shape=[jax.Shap...  45.7 us
    pallas_call x1, Pallas kernels, attend(): pl.pallas_call(attend_kernel, grid_spec=pltpu.PrefetchScalarGridSpec(num_...  28.7 us
    unnamed x5, local copies, waits for them, and re-layouts  23.3 us

profile of v2, /device:TPU:97, one launch (start us, length us, event | category | flops | bytes accessed | tf_op | source)
XLA Modules:
  0.0 278.3 jit_solution(2121094647230726090)
XLA Ops:
  0.6 0.0 copy-start
  0.7 1.5 dynamic_slice.6.len_ref
  2.1 0.1 copy-done
  2.2 2.3 convolution_convert_fusion.1
  4.6 3.0 %convolution_convert_fusion = bf16[64,128]{1,0:T(8,128)(2,1)} fusion(bf16[8192,128]{1,0:T(8,128)(2,1)} %param.11, bf16[2048,8192]{1,0:T(8,128)(2,1)} %param.8, s32[]{:T(128)S(6)} %select_n.4), kind=kOutput, calls=%fused_computation | convolution fusion | flops 134225920 | bytes 3162116 | tf_op jit(solution)/shard_map/dot_general | solution.py:422
  7.6 45.7 %project_queries.1 = (bf16[4,4,64,512]{3,2,1,0:T(8,128)(2,1)}, bf16[4,2,256,1024]{3,2,1,0:T(8,128)(2,1)}, bf16[4,2,256,1024]{3,2,1,0:T(8,128)(2,1)}) custom-call(bf16[4,4,2,64,8192]{4,3,2,1,0:T(8,128)(2,1)} %bitcast.15, bf16[8192,256]{1,0:T(8,128)(2,1)} %wq_ref.1, bf16[256,8192]{1,0:T(8,128)(2,1)} %wo_ref.1), custom_call_target="tpu_custom_call" | custom-call | tf_op jit(solution)/shard_map/project_queries/pallas_call | solution.py:364
  53.3 1.3 reshape.31
  54.6 1.6 copy.11
  56.2 28.7 %attend.1 = (bf16[64,512,128]{2,1,0:T(8,128)(2,1)}, bf16[64,512,128]{2,1,0:T(8,128)(2,1)}, bf16[64,64,128]{2,1,0:T(8,128)(2,1)}) custom-call(s32[64]{0:T(128)} %dynamic_slice.6.len_ref, bf16[64,64,128]{2,1,0:T(8,128)(2,1)} %bitcast.18, bf16[16,4,128]{2,1,0:T(4,128)(2,1)} %bitcast.21, bf16[16,4,128]{2,1,0:T(4,128)(2,1)} %bitcast.22, ...), custom_call_target="tpu_custom_call" | custom-call | flops 1073741824 | bytes 33554432 | tf_op jit(solution)/shard_map/attend/pallas_call | solution.py:51
  84.9 1.7 copy.14
  86.6 1.2 reshape.36.ctx_ref
  87.8 167.1 %project_context.1 = bf16[4,4,2,64,8192]{4,3,2,1,0:T(8,128)(2,1)} custom-call(bf16[4,4,64,512]{3,2,1,0:T(8,128)(2,1)} %reshape.36.ctx_ref, bf16[4,2,256,1024]{3,2,1,0:T(8,128)(2,1)} %get-tuple-element.11.wa_ref, bf16[4,2,256,1024]{3,2,1,0:T(8,128)(2,1)} %get-tuple-element.12.wb_ref, bf16[4,4,2,64,8192]{4,3,2,1,0:T(8,128)(2,1)} %bitcast.16), custom_call_target="tpu_custom_call" | custom-call | tf_op jit(solution)/shard_map/project_context/pallas_call | solution.py:386
  255.0 0.0 copy-start.1
  255.0 23.1 %copy.16 = bf16[2048,8192]{1,0:T(8,128)(2,1)} copy(bf16[2048,8192]{1,0:T(8,128)(2,1)} %bitcast.17) | data formatting | bytes 67108864
  278.1 0.0 copy-done.1
Async XLA Ops:
  0.6 1.6 copy-start
  255.0 23.1 %copy-start.1 = (bf16[8192,128]{1,0:T(8,128)(2,1)S(1)}, bf16[8192,128]{1,0:T(8,128)(2,1)}, u32[]{:S(2)}) copy-start(bf16[8192,128]{1,0:T(8,128)(2,1)} %param.10) | copy-start | bytes 6291460

commit v3 on v2

v3 whole, which is shorter than its diff:
```python
import functools
import math
import jax
import jax.numpy as jnp
from jax import lax
from jax.experimental import pallas as pl
from jax.experimental.pallas import tpu as pltpu
from jax.sharding import PartitionSpec as P

CHUNK = 16


def attend_rows(query, keys, values, row_lens, score_scale):
    seq_len = keys[0].shape[0]
    positions = lax.broadcasted_iota(jnp.int32, (1, seq_len), 1)
    scores = [
        lax.dot_general(q, k, (((1,), (1,)), ((), ())), preferred_element_type=jnp.float32) + jnp.where(positions <= n, 0.0, -jnp.inf)
        for q, k, n in zip(query, keys, row_lens)
    ]
    weights = [jnp.exp2((s - jnp.max(s, axis=1, keepdims=True)) * (score_scale * math.log2(math.e))) for s in scores]
    sums = [jnp.sum(e, axis=1, keepdims=True) for e in weights]
    return [(jnp.dot(e.astype(jnp.bfloat16), v, preferred_element_type=jnp.float32) / t).astype(jnp.bfloat16) for e, v, t in zip(weights, values, sums)]


def attend_kernel(len_ref, q_hbm, new_ref, k_hbm, v_hbm, ko_hbm, vo_hbm, ctx_ref, q_ref, k_ref, v_ref, q_sem, in_sems, out_sems):
    n, seq_len, head_dim = k_ref.shape
    tile = math.gcd(seq_len, 16)
    first = lax.axis_index('model') * n

    def loads(i):
        part = pl.ds(i * CHUNK, CHUNK)
        return [pltpu.make_async_copy(src.at[part], dst.at[part], in_sems.at[j, i]) for j, (src, dst) in enumerate(((k_hbm, k_ref), (v_hbm, v_ref)))]

    def stores(i):
        part = pl.ds(i * CHUNK, CHUNK)
        return [pltpu.make_async_copy(src.at[part], dst.at[part], out_sems.at[j, i]) for j, (src, dst) in enumerate(((k_ref, ko_hbm), (v_ref, vo_hbm)))]

    q_copy = pltpu.make_async_copy(q_hbm, q_ref, q_sem)
    q_copy.start()
    for i in range(n // CHUNK):
        for copy in loads(i):
            copy.start()
    q_copy.wait()

    @pl.loop(0, n // CHUNK)
    def _(i):
        for copy in loads(i):
            copy.wait()
        rows = [i * CHUNK + r for r in range(CHUNK)]
        lens = [len_ref[first + r] for r in rows]
        for r, row_len in zip(rows, lens):
            base = pl.multiple_of((row_len // tile) * tile, tile)
            pick = lax.broadcasted_iota(jnp.int32, (tile, head_dim), 0) == row_len - base
            for j, ref in enumerate((k_ref, v_ref)):
                new = jnp.broadcast_to(new_ref[j, pl.ds(r, 1), :], (tile, head_dim))
                old = ref[r, pl.ds(base, tile), :].astype(jnp.float32)
                ref[r, pl.ds(base, tile), :] = jnp.where(pick, new, old).astype(jnp.bfloat16)
        out = attend_rows([q_ref[r] for r in rows], [k_ref[r] for r in rows], [v_ref[r] for r in rows], lens, head_dim ** -0.5)
        for r, ctx in zip(rows, out):
            ctx_ref[r] = ctx
        for copy in stores(i):
            copy.start()

    @pl.loop(0, n // CHUNK)
    def _(i):
        for copy in stores(i):
            copy.wait()


def attend(lens, query, new, key_cache, value_cache):
    n, seq_len, head_dim = key_cache.shape
    n_heads = query.shape[1]
    return pl.pallas_call(
        attend_kernel,
        in_specs=[pl.BlockSpec(memory_space=pltpu.SMEM), ANY, VMEM, ANY, ANY],
        out_specs=[ANY, ANY, VMEM],
        out_shape=[
            jax.ShapeDtypeStruct(key_cache.shape, key_cache.dtype),
            jax.ShapeDtypeStruct(value_cache.shape, value_cache.dtype),
            jax.ShapeDtypeStruct(query.shape, jnp.bfloat16),
        ],
        scratch_shapes=[
            pltpu.VMEM(query.shape, jnp.bfloat16),
            pltpu.VMEM(key_cache.shape, jnp.bfloat16),
            pltpu.VMEM(value_cache.shape, jnp.bfloat16),
            pltpu.SemaphoreType.DMA(()),
            pltpu.SemaphoreType.DMA((2, n // CHUNK)),
            pltpu.SemaphoreType.DMA((2, n // CHUNK)),
        ],
        compiler_params=pltpu.CompilerParams(vmem_limit_bytes=63 << 20),
        cost_estimate=pl.CostEstimate(flops=4 * n * n_heads * seq_len * head_dim, bytes_accessed=8 * n * seq_len * head_dim, transcendentals=0),
        name='attend',
    )(lens, query, new, key_cache, value_cache)


ANY = pl.BlockSpec(memory_space=pl.ANY)
VMEM = pl.BlockSpec(memory_space=pltpu.VMEM)


MESH = pl.DeviceIdType.MESH
CORES = 2


class Moves:
    def __init__(self, send_sems, recv_sems):
        self.send_sems, self.recv_sems = send_sems, recv_sems
        self.count, self.copies, self.unsent = 0, {}, []

    def send(self, key, src, dst, device):
        copy = pltpu.make_async_remote_copy(src_ref=src, dst_ref=dst, send_sem=self.send_sems.at[self.count], recv_sem=self.recv_sems.at[self.count], device_id={'model': device}, device_id_type=MESH)
        copy.start()
        self.count += 1
        self.copies[key] = copy
        self.unsent.append(copy)

    def local(self, key, src, dst):
        copy = pltpu.make_async_copy(src, dst, self.send_sems.at[self.count])
        copy.start()
        self.count += 1
        self.copies[key] = copy

    def got(self, key):
        self.copies.pop(key).wait_recv()

    def done(self, key):
        self.copies.pop(key).wait()

    def finish(self):
        for copy in self.unsent:
            copy.wait_send()


def place(side):
    me = lax.axis_index('model')
    return me // (CORES * side), lax.rem(me // CORES, side), lax.rem(me, CORES)


def greet(devices):
    barrier = pltpu.get_barrier_semaphore()
    for device in devices:
        pl.semaphore_signal(barrier, inc=1, device_id={'model': device}, device_id_type=MESH)
    pl.semaphore_wait(barrier, len(devices))


def columns(start, width):
    return pl.ds(pl.multiple_of(start * width, width), width)


def query_kernel(side, hid_ref, wq_ref, wo_ref, wk_ref, wv_ref, q_ref, wa_ref, wb_ref, new_ref, wq_all, hid, q_buf, acc, w_new, own_w, load_sems, send_sems, recv_sems):
    y, x, c = place(side)
    rows, dim = hid_ref.shape[3:]
    half = wq_ref.shape[1]
    w_rows = wo_ref.shape[0]
    width = wo_ref.shape[1] // (2 * side)
    w_refs = (wa_ref, wb_ref)
    step = lambda a, d: lax.rem(a + d + side, side)
    dev = lambda yy, xx: (yy * side + xx) * CORES + c
    other = (y * side + x) * CORES + 1 - c
    peers = [(dy, dx) for dy in range(side) for dx in range(side) if dy or dx]
    mv = Moves(send_sems, recv_sems)
    order = list(range(1, side)) + [0]
    depth, pair = min(2048, dim), side // 2

    def loads(k):
        part = columns(k, depth)
        pairs = [(wq_ref.at[part], wq_all.at[c, part])] + [(hid_ref.at[step(y, dy), :, c, :, part], hid.at[i, :, :, part]) for i, dy in enumerate(order)]
        return [pltpu.make_async_copy(src, dst, load_sems.at[j, k]) for j, (src, dst) in enumerate(pairs)]

    for k in range(dim // depth):
        for copy in loads(k):
            copy.start()
    greet([dev(step(y, dy), step(x, dx)) for dy, dx in peers] + [other])
    mv.send('wq', wq_ref, wq_all.at[c], other)
    along = ((x, lambda u: dev(y, u)), (y, lambda u: dev(u, x)))
    wcols = lambda t, u: columns(t * side + u, width)
    for t, (u, at) in enumerate(along):
        mv.send(('w', t, 2), wo_ref.at[:, wcols(t, step(u, 2))], w_refs[t].at[u, c], at(step(u, 2)))
        for d in (1, 3):
            mv.send(('w', t, d), wo_ref.at[:, wcols(t, step(u, d))], w_refs[t].at[u, c], at(step(u, d)))
        mv.local(('w_own', t), wo_ref.at[:, wcols(t, u)], own_w.at[t])
    for j, ref in enumerate((wk_ref, wv_ref)):
        mv.local(('w_new', j), ref, w_new.at[j])

    def gain(h, core, part):
        acc[h] += jnp.dot(hid[pl.ds(h * pair, pair), :, :, part].reshape(pair * side * rows, depth), wq_all[core, part, :], preferred_element_type=jnp.float32)

    def store(h, core):
        q_buf[pl.ds(h * pair, pair), :, :, columns(core, half)] = acc[h].astype(jnp.bfloat16).reshape(pair, side, rows, half)
        acc[h] = jnp.zeros_like(acc[h])

    acc[...] = jnp.zeros_like(acc)

    @pl.loop(0, dim // depth)
    def _(k):
        for copy in loads(k):
            copy.wait()
        for h in range(2):
            gain(h, c, columns(k, depth))

    for h in range(2):
        store(h, c)

    def project(h):
        @pl.loop(0, dim // depth)
        def _(k):
            gain(h, 1 - c, columns(k, depth))

        store(h, 1 - c)

    for t, (u, at) in enumerate(along):
        mv.done(('w_own', t))
        mv.local(('w_put', t), own_w.at[t], w_refs[t].at[u, c])
        mv.send(('wS', t, 0), own_w.at[t], w_refs[t].at[u, c], other)
    mv.got('wq')
    for i, dy in enumerate(order):
        if i % pair == 0:
            project(i // pair)
        for dx in [d for d in (2, 1, 3, 0)][:side]:
            if dy or dx:
                mv.send(('q', dy, dx), q_buf.at[i, step(x, dx)], q_ref.at[y, x], dev(step(y, dy), step(x, dx)))
            else:
                mv.local('q_own', q_buf.at[i, x], q_ref.at[y, x])
    for j in range(2):
        mv.done(('w_new', j))
        new = jnp.zeros((rows, w_new.shape[2]), jnp.float32)
        for k in range(0, dim, depth):
            new += jnp.dot(hid[side - 1, x, :, k:k + depth], w_new[j, k:k + depth, :], preferred_element_type=jnp.float32)
        new_ref[j] = new.astype(jnp.bfloat16).astype(jnp.float32)
    for d in (2, 1, 3):
        for t, (u, at) in enumerate(along):
            mv.got(('w', t, d))
            tile = w_refs[t].at[step(u, -d), c]
            mv.send(('wS', t, d), tile, tile, other)
    for dy, dx in peers:
        mv.got(('q', dy, dx))
    mv.done('q_own')
    for t in range(2):
        mv.done(('w_put', t))
        for d in range(side):
            mv.got(('wS', t, d))
    mv.finish()


def output_kernel(side, ctx_ref, wa_ref, wb_ref, hid_ref, out_ref, held, w_buf, acc, keep, part, first, second, final, send_sems, recv_sems):
    y, x, c = place(side)
    rows, depth = ctx_ref.shape[2:]
    width = w_buf.shape[-1]
    step = lambda a, d: lax.rem(a + d + side, side)
    dev = lambda yy, xx: (yy * side + xx) * CORES + c
    other = (y * side + x) * CORES + 1 - c
    spots = ((y, x), (x, y))
    at = lambda t, v, u: dev(v, u) if t == 0 else dev(u, v)
    ctx_of = lambda t, v: ctx_ref.at[v] if t == 0 else ctx_ref.at[:, v]
    greet([dev(y, step(x, d)) for d in range(1, side)] + [dev(step(y, d), x) for d in range(1, side)] + [other])
    mv = Moves(send_sems, recv_sems)
    both = range(2)

    def view(ref, t, v, g, us=None):
        us = slice(None) if us is None else us
        cols = columns(t * side + g, width)
        return ref.at[v, us, c, :, cols] if t == 0 else ref.at[us, v, c, :, cols]

    for t in both:
        v, u = spots[t]
        mv.send(('a', t, 2), ctx_of(t, step(v, 2)), held.at[t, u, v], at(t, step(v, 2), u))
    for t in both:
        v, u = spots[t]
        for d in (1, 3):
            mv.send(('a', t, d), ctx_of(t, step(v, d)), held.at[t, u, v], at(t, step(v, d), u))
        mv.send(('gR', t, 0), ctx_of(t, v), held.at[t, u, v], at(t, v, step(u, 1)))
        mv.send(('gL', t, 0), ctx_of(t, v), held.at[t, u, v], at(t, v, step(u, -1)))
    for t in both:
        v, u = spots[t]
        mv.local(('w', t), (wa_ref, wb_ref)[t], w_buf.at[t])
        mv.local(('hid', t), view(hid_ref, t, v, u), final.at[t])

    def spread(t, p, tag):
        v, u = spots[t]
        slot = held.at[t, u, step(v, -p)]
        mv.send(('g' + tag, t, p), slot, slot, at(t, v, step(u, 1 if tag == 'R' else -1)))

    def forward(t, p, tag):
        v, u = spots[t]
        mv.got(('g' + tag, t, p))
        slot = held.at[t, step(u, -1 if tag == 'R' else 1), step(v, -p)]
        mv.send(('f', t, p), slot, slot, at(t, v, step(u, 1 if tag == 'R' else -1)))

    for t in both:
        mv.got(('a', t, 2))
        spread(t, 2, 'R')
        mv.got(('a', t, 1))
        spread(t, 1, 'L')
        spread(t, 2, 'L')
        spread(t, 1, 'R')
    for t in both:
        forward(t, 2, 'R')
        forward(t, 1, 'L')
        mv.got(('a', t, 3))
        spread(t, 3, 'R')
        spread(t, 3, 'L')
    for t in both:
        forward(t, 0, 'R')
    for t in both:
        mv.done(('w', t))

    def product(t, p):
        v, u = spots[t]
        total = None
        for k in range(side):
            pieces = []
            for d in range(side):
                if p == 0 and d == 0:
                    pieces.append(ctx_ref[v, k] if t == 0 else ctx_ref[k, v])
                else:
                    pieces.append(held[t, step(u, d), step(v, -p), k])
            one = jnp.dot(jnp.concatenate(pieces, axis=0), w_buf[t, k].reshape(depth, width), preferred_element_type=jnp.float32)
            total = one if total is None else total + one
        acc[t] = total.reshape(side, rows, width)

    upper, lower = pl.ds(0, side // 2), pl.ds(side // 2, side // 2)
    for t in both:
        v, u = spots[t]
        mv.got(('gL', t, 2))
        mv.got(('f', t, 2))
        product(t, 2)
        part[t, 2] = acc[t].astype(jnp.bfloat16)
        mv.send(('r1R', t), part.at[t, 2, upper], first.at[t, 0], at(t, step(v, 1), u))
        mv.send(('r1L', t), part.at[t, 2, lower], first.at[t, 1], at(t, step(v, -1), u))
    for t in both:
        forward(t, 3, 'L')
    sides = ((1, upper, lower, 'L', 1), (3, lower, upper, 'R', 0))
    for p, now, later, tag, d in sides:
        for t in both:
            v, u = spots[t]
            mv.got(('gR', t, p))
            mv.got(('f', t, p))
            product(t, p)
            part[t, p, now] = acc[t, now].astype(jnp.bfloat16)
            mv.send(('r2' + tag, t), part.at[t, p, now], second.at[t, d, now], at(t, step(v, -p), u))
            keep[t, d] = acc[t, later]
    for p, now, later, tag, d in sides:
        for t in both:
            v, u = spots[t]
            mv.got(('r1' + tag, t))
            part[t, p, later] = (keep[t, d] + first[t, d].astype(jnp.float32)).astype(jnp.bfloat16)
            mv.send(('r3' + tag, t), part.at[t, p, later], second.at[t, d, later], at(t, step(v, -p), u))
    for t in both:
        mv.got(('gL', t, 0))
        mv.got(('f', t, 0))
        product(t, 0)
    for t in both:
        v, u = spots[t]
        for tag in 'RL':
            mv.got(('r2' + tag, t))
            mv.got(('r3' + tag, t))
        mv.done(('hid', t))
        for d in range(side):
            us = step(u, d)
            y_sum = acc[t, d] + second[t, 0, d].astype(jnp.float32) + second[t, 1, d].astype(jnp.float32)
            final[t, us] = (final[t, us].astype(jnp.float32) + y_sum).astype(jnp.bfloat16)
        mine = view(out_ref, t, v, u)
        mv.send(('oR', t), final.at[t], mine, at(t, v, step(u, 1)))
        mv.send(('oL', t), final.at[t], mine, at(t, v, step(u, -1)))
        mv.send(('pR', t, 0), final.at[t], mine, at(t, step(v, 1), u))
        mv.send(('pL', t, 0), final.at[t], mine, at(t, step(v, -1), u))
        mv.local(('own', t), final.at[t], mine)
        mv.send(('s', t, 0, 0), final.at[t], mine, other)
    for t in both:
        v, u = spots[t]
        mv.got(('oR', t))
        half = view(out_ref, t, v, step(u, -1), upper)
        mv.send(('o2R', t), half, half, at(t, v, step(u, 1)))
        mv.got(('oL', t))
        half = view(out_ref, t, v, step(u, 1), lower)
        mv.send(('o2L', t), half, half, at(t, v, step(u, -1)))
    offsets = (0, -1, 1, 2)
    for g in (1, 2, 3):
        for t in both:
            v, u = spots[t]
            if g == 3:
                mv.got(('o2R', t))
                mv.got(('o2L', t))
            piece = view(out_ref, t, v, step(u, offsets[g]))
            mv.send(('pR', t, g), piece, piece, at(t, step(v, 1), u))
            mv.send(('pL', t, g), piece, piece, at(t, step(v, -1), u))
            mv.send(('s', t, 0, g), piece, piece, other)
    for g in range(4):
        for t in both:
            v, u = spots[t]
            mv.got(('pR', t, g))
            piece = view(out_ref, t, step(v, -1), step(u, offsets[g]))
            if g in (0, 2):
                mv.send(('z', t, g), piece, piece, at(t, step(v, 1), u))
            mv.send(('s', t, 1, g), piece, piece, other)
            mv.got(('pL', t, g))
            piece = view(out_ref, t, step(v, 1), step(u, offsets[g]))
            if g in (1, 3):
                mv.send(('z', t, g), piece, piece, at(t, step(v, -1), u))
            mv.send(('s', t, 2, g), piece, piece, other)
    for g in range(4):
        for t in both:
            v, u = spots[t]
            mv.got(('z', t, g))
            piece = view(out_ref, t, step(v, 2), step(u, offsets[g]))
            mv.send(('s', t, 3, g), piece, piece, other)
    for t in both:
        mv.done(('own', t))
        for i in range(4):
            for g in range(4):
                mv.got(('s', t, i, g))
    mv.finish()


def sems(n):
    return [pltpu.SemaphoreType.DMA((n,)), pltpu.SemaphoreType.DMA((n,))]


def project_queries(side, hidden, w_query, w_out, w_key, w_value):
    rows, dim = hidden.shape[3:]
    half = w_query.shape[1]
    w_rows, width = w_out.shape[0], w_out.shape[1] // (2 * side)
    bf16 = jnp.bfloat16
    tile = jax.ShapeDtypeStruct((side, CORES, w_rows, width), bf16)
    return pl.pallas_call(
        functools.partial(query_kernel, side),
        out_shape=[jax.ShapeDtypeStruct((side, side, rows, CORES * half), bf16), tile, tile, jax.ShapeDtypeStruct((2, rows, w_key.shape[1]), jnp.float32)],
        in_specs=[ANY] * 5,
        out_specs=[ANY] * 3 + [VMEM],
        scratch_shapes=[
            pltpu.VMEM((CORES, dim, half), bf16),
            pltpu.VMEM((side, side, rows, dim), bf16),
            pltpu.VMEM((side, side, rows, CORES * half), bf16),
            pltpu.VMEM((2, side // 2 * side * rows, half), jnp.float32),
            pltpu.VMEM((2,) + w_key.shape, bf16),
            pltpu.VMEM((2, w_rows, width), bf16),
            pltpu.SemaphoreType.DMA((1 + side, dim // min(2048, dim))),
        ] + sems(64),
        compiler_params=pltpu.CompilerParams(collective_id=0, has_side_effects=True, vmem_limit_bytes=63 << 20),
        name='project_queries',
    )(hidden, w_query, w_out, w_key, w_value)


def project_context(side, context, w_a, w_b, hidden):
    rows, depth = context.shape[2:]
    width = w_a.shape[-1]
    bf16, f32 = jnp.bfloat16, jnp.float32
    return pl.pallas_call(
        functools.partial(output_kernel, side),
        out_shape=pltpu.VMEM(hidden.shape, bf16),
        in_specs=[VMEM, ANY, ANY, ANY],
        out_specs=ANY,
        scratch_shapes=[
            pltpu.VMEM((2, side, side, side, rows, depth), bf16),
            pltpu.VMEM((2,) + w_a.shape, bf16),
            pltpu.VMEM((2, side, rows, width), f32),
            pltpu.VMEM((2, 2, side // 2, rows, width), f32),
            pltpu.VMEM((2, 4, side, rows, width), bf16),
            pltpu.VMEM((2, 2, side // 2, rows, width), bf16),
            pltpu.VMEM((2, 2, side, rows, width), bf16),
            pltpu.VMEM((2, side, rows, width), bf16),
        ] + sems(128),
        compiler_params=pltpu.CompilerParams(collective_id=1, has_side_effects=True, vmem_limit_bytes=30 << 20),
        name='project_context',
    )(context, w_a, w_b, hidden)


def put_kernel(src_ref, dst_ref, copy_sems):
    n = src_ref.shape[0] * src_ref.shape[1]
    side = src_ref.shape[1]
    copies = [pltpu.make_async_copy(src_ref.at[i // side, i % side], dst_ref.at[i // side, i % side], copy_sems.at[i]) for i in range(n)]
    for copy in copies:
        copy.start()
    for copy in copies:
        copy.wait()


def put(result):
    return pl.pallas_call(
        put_kernel,
        out_shape=jax.ShapeDtypeStruct(result.shape, result.dtype),
        in_specs=[ANY],
        out_specs=ANY,
        scratch_shapes=[pltpu.SemaphoreType.DMA((result.shape[0] * result.shape[1],))],
        compiler_params=pltpu.CompilerParams(vmem_limit_bytes=1 << 20),
        name='put',
    )(result)


def solution(mesh):
    side = math.isqrt(mesh.shape['model'] // CORES)

    def group_step(hidden, w_query, w_key, w_value, w_out, key_cache, value_cache, lengths):
        n_rows, dim = hidden.shape
        local_rows = key_cache.shape[0]
        head_dim = key_cache.shape[2]
        chip_cols = CORES * w_query.shape[1]
        n_heads = side * side * chip_cols // head_dim
        hidden_tiles = hidden.reshape(side, side, CORES, local_rows, dim)
        query, w_a, w_b, new = project_queries(side, hidden_tiles, w_query, w_out, w_key, w_value)
        query = query.reshape(side * side, local_rows, chip_cols // head_dim, head_dim).transpose(1, 0, 2, 3).reshape(local_rows, n_heads, head_dim)
        key_upd, value_upd, context = attend(lengths, query, new, key_cache, value_cache)
        context = context.reshape(local_rows, side * side, chip_cols // head_dim, head_dim).transpose(1, 0, 2, 3).reshape(side, side, local_rows, chip_cols)
        hidden_out = put(project_context(side, context, w_a, w_b, hidden_tiles))
        return hidden_out.reshape(n_rows, dim), key_upd, value_upd

    row_spec = P('replica', None)
    cache_spec = P(('replica', 'model'), None, None)
    return jax.shard_map(group_step, mesh=mesh, in_specs=(row_spec, P(None, 'model'), P(None, None), P(None, None), P('model', None), cache_spec, cache_spec, P('replica')), out_specs=(row_spec, cache_spec, cache_spec), check_vma=False)
```

time: 279 us -> 242 us (0.87)
  local copies, waits for them, and re-layouts: 30.6 us -> 5.82 us
  Pallas kernels: 242 us -> 235 us
  matrix products: 5.33 us -> 0 us
    unnamed x5 -> x0, local copies, waits for them, and re-layouts: 23.3 us -> none
    pallas_call x2 -> x3, Pallas kernels: 196 us -> 188 us  [the longest x1 163 us: project_context(): pl.pallas_call(functools.partial(output_kernel, side), out_shape=pltpu.VM...]
    dot_general x2 -> x0, matrix products: 5.33 us -> none  [the longest x1 3.01 us: group_step(): jnp.dot(hidden_local, w_value, preferred_element_type=jnp.float32)]
where the time goes in v3:
time: 242 us
  Pallas kernels  235 us (97%)
  local copies, waits for them, and re-layouts  5.82 us (2%)
    pallas_call x1, Pallas kernels, project_context(): pl.pallas_call(functools.partial(output_kernel, side), out_shape=pltpu.VM...  163 us
    pallas_call x1, Pallas kernels, project_queries(): pl.pallas_call(functools.partial(query_kernel, side), out_shape=[jax.Shap...  47.1 us
    pallas_call x1, Pallas kernels, attend(): pl.pallas_call(attend_kernel, in_specs=[pl.BlockSpec(memory_space=pltpu.S...  14.4 us
    pallas_call x1, Pallas kernels, put(): pl.pallas_call(put_kernel, out_shape=jax.ShapeDtypeStruct(result.shape, r...  11 us

profile of v3, /device:TPU:97, one launch (start us, length us, event | category | flops | bytes accessed | tf_op | source)
XLA Modules:
  0.0 242.1 jit_solution(16772744062206403244)
XLA Ops:
  0.6 47.1 %project_queries.1 = (bf16[4,4,64,512]{3,2,1,0:T(8,128)(2,1)}, bf16[4,2,256,1024]{3,2,1,0:T(8,128)(2,1)}, bf16[4,2,256,1024]{3,2,1,0:T(8,128)(2,1)}, f32[2,64,128]{2,1,0:T(8,128)}) custom-call(bf16[4,4,2,64,8192]{4,3,2,1,0:T(8,128)(2,1)} %bitcast.11, bf16[8192,256]{1,0:T(8,128)(2,1)} %wq_ref.1, bf16[256,8192]{1,0:T(8,128)(2,1)} %wo_ref.1, ...), custom_call_target="tpu_custom_call" | custom-call | tf_op jit(solution)/shard_map/project_queries/pallas_call | solution.py:424
  47.7 1.3 reshape.25
  49.1 1.6 copy.11
  50.6 14.4 %attend.1 = (bf16[64,512,128]{2,1,0:T(8,128)(2,1)}, bf16[64,512,128]{2,1,0:T(8,128)(2,1)}, bf16[64,64,128]{2,1,0:T(8,128)(2,1)}) custom-call(s32[2048]{0:T(1024)} %len_ref.1, bf16[64,64,128]{2,1,0:T(8,128)(2,1)} %bitcast.14, f32[2,64,128]{2,1,0:T(8,128)} %get-tuple-element.11.new_ref, bf16[64,512,128]{2,1,0:T(8,128)(2,1)} %k_hbm.1, bf16[64,512,128]{2,1,0:T(8,128)(2,1)} %v_hbm.1), custom_call_target="tpu_custom_call" | custom-call | flops 1073741824 | bytes 33554432 | tf_op jit(solution)/shard_map/attend/pallas_call | solution.py:73
  65.1 1.7 copy.14
  66.8 1.2 reshape.28.ctx_ref
  68.0 162.8 %project_context.1.src_ref = bf16[4,4,2,64,8192]{4,3,2,1,0:T(8,128)(2,1)S(1)} custom-call(bf16[4,4,64,512]{3,2,1,0:T(8,128)(2,1)} %reshape.28.ctx_ref, bf16[4,2,256,1024]{3,2,1,0:T(8,128)(2,1)} %get-tuple-element.13.wa_ref, bf16[4,2,256,1024]{3,2,1,0:T(8,128)(2,1)} %get-tuple-element.14.wb_ref, bf16[4,4,2,64,8192]{4,3,2,1,0:T(8,128)(2,1)} %bitcast.12), custom_call_target="tpu_custom_call" | custom-call | tf_op jit(solution)/shard_map/project_context/pallas_call | solution.py:447
  230.8 11.0 %put.1 = bf16[4,4,2,64,8192]{4,3,2,1,0:T(8,128)(2,1)} custom-call(bf16[4,4,2,64,8192]{4,3,2,1,0:T(8,128)(2,1)S(1)} %project_context.1.src_ref), custom_call_target="tpu_custom_call" | custom-call | tf_op jit(solution)/shard_map/put/pallas_call | solution.py:478

commit v4 on v3

--- a/solution.py
+++ b/solution.py
@@ -10,19 +10,23 @@
 CHUNK = 16
 
 
-def attend_rows(query, keys, values, row_lens, score_scale):
-    seq_len = keys[0].shape[0]
-    positions = lax.broadcasted_iota(jnp.int32, (1, seq_len), 1)
-    scores = [
-        lax.dot_general(q, k, (((1,), (1,)), ((), ())), preferred_element_type=jnp.float32) + jnp.where(positions <= n, 0.0, -jnp.inf)
+def attend_rows(query, keys, values, new_keys, new_values, row_lens, score_scale):
+    positions = lax.broadcasted_iota(jnp.int32, (1, keys[0].shape[0]), 1)
+    factor = score_scale * math.log2(math.e)
+    old = [
+        lax.dot_general(q.astype(jnp.bfloat16), k, (((1,), (1,)), ((), ())), preferred_element_type=jnp.float32) + jnp.where(positions < n, 0.0, -jnp.inf)
         for q, k, n in zip(query, keys, row_lens)
     ]
-    weights = [jnp.exp2((s - jnp.max(s, axis=1, keepdims=True)) * (score_scale * math.log2(math.e))) for s in scores]
-    sums = [jnp.sum(e, axis=1, keepdims=True) for e in weights]
-    return [(jnp.dot(e.astype(jnp.bfloat16), v, preferred_element_type=jnp.float32) / t).astype(jnp.bfloat16) for e, v, t in zip(weights, values, sums)]
-
-
-def attend_kernel(len_ref, q_hbm, new_ref, k_hbm, v_hbm, ko_hbm, vo_hbm, ctx_ref, q_ref, k_ref, v_ref, q_sem, in_sems, out_sems):
+    own = [jnp.sum(q * k, axis=1, keepdims=True) for q, k in zip(query, new_keys)]
+    tops = [jnp.maximum(jnp.max(s, axis=1, keepdims=True), o) for s, o in zip(old, own)]
+    old = [jnp.exp2((s - t) * factor) for s, t in zip(old, tops)]
+    own = [jnp.exp2((o - t) * factor) for o, t in zip(own, tops)]
+    sums = [jnp.sum(s, axis=1, keepdims=True) + o for s, o in zip(old, own)]
+    mixed = [jnp.dot(s.astype(jnp.bfloat16), v, preferred_element_type=jnp.float32) for s, v in zip(old, values)]
+    return [(m + o.astype(jnp.bfloat16).astype(jnp.float32) * v) / t for m, o, v, t in zip(mixed, own, new_values, sums)]
+
+
+def update_kernel(len_ref, new_ref, k_hbm, v_hbm, ko_hbm, vo_hbm, k_ref, v_ref, in_sems, out_sems):
     n, seq_len, head_dim = k_ref.shape
     tile = math.gcd(seq_len, 16)
     first = lax.axis_index('model') * n
@@ -35,29 +39,23 @@
         part = pl.ds(i * CHUNK, CHUNK)
         return [pltpu.make_async_copy(src.at[part], dst.at[part], out_sems.at[j, i]) for j, (src, dst) in enumerate(((k_ref, ko_hbm), (v_ref, vo_hbm)))]
 
-    q_copy = pltpu.make_async_copy(q_hbm, q_ref, q_sem)
-    q_copy.start()
     for i in range(n // CHUNK):
         for copy in loads(i):
             copy.start()
-    q_copy.wait()
 
     @pl.loop(0, n // CHUNK)
     def _(i):
         for copy in loads(i):
             copy.wait()
-        rows = [i * CHUNK + r for r in range(CHUNK)]
-        lens = [len_ref[first + r] for r in rows]
-        for r, row_len in zip(rows, lens):
+        for r in range(CHUNK):
+            r = i * CHUNK + r
+            row_len = len_ref[first + r]
             base = pl.multiple_of((row_len // tile) * tile, tile)
             pick = lax.broadcasted_iota(jnp.int32, (tile, head_dim), 0) == row_len - base
             for j, ref in enumerate((k_ref, v_ref)):
                 new = jnp.broadcast_to(new_ref[j, pl.ds(r, 1), :], (tile, head_dim))
                 old = ref[r, pl.ds(base, tile), :].astype(jnp.float32)
                 ref[r, pl.ds(base, tile), :] = jnp.where(pick, new, old).astype(jnp.bfloat16)
-        out = attend_rows([q_ref[r] for r in rows], [k_ref[r] for r in rows], [v_ref[r] for r in rows], lens, head_dim ** -0.5)
-        for r, ctx in zip(rows, out):
-            ctx_ref[r] = ctx
         for copy in stores(i):
             copy.start()
 
@@ -67,30 +65,22 @@
             copy.wait()
 
 
-def attend(lens, query, new, key_cache, value_cache):
-    n, seq_len, head_dim = key_cache.shape
-    n_heads = query.shape[1]
+def update(lens, new, key_cache, value_cache):
+    n = key_cache.shape[0]
     return pl.pallas_call(
-        attend_kernel,
-        in_specs=[pl.BlockSpec(memory_space=pltpu.SMEM), ANY, VMEM, ANY, ANY],
-        out_specs=[ANY, ANY, VMEM],
-        out_shape=[
-            jax.ShapeDtypeStruct(key_cache.shape, key_cache.dtype),
-            jax.ShapeDtypeStruct(value_cache.shape, value_cache.dtype),
-            jax.ShapeDtypeStruct(query.shape, jnp.bfloat16),
-        ],
+        update_kernel,
+        in_specs=[pl.BlockSpec(memory_space=pltpu.SMEM), VMEM, ANY, ANY],
+        out_specs=[ANY] * 2,
+        out_shape=[jax.ShapeDtypeStruct(x.shape, x.dtype) for x in (key_cache, value_cache)],
         scratch_shapes=[
-            pltpu.VMEM(query.shape, jnp.bfloat16),
             pltpu.VMEM(key_cache.shape, jnp.bfloat16),
             pltpu.VMEM(value_cache.shape, jnp.bfloat16),
-            pltpu.SemaphoreType.DMA(()),
             pltpu.SemaphoreType.DMA((2, n // CHUNK)),
             pltpu.SemaphoreType.DMA((2, n // CHUNK)),
         ],
         compiler_params=pltpu.CompilerParams(vmem_limit_bytes=63 << 20),
-        cost_estimate=pl.CostEstimate(flops=4 * n * n_heads * seq_len * head_dim, bytes_accessed=8 * n * seq_len * head_dim, transcendentals=0),
-        name='attend',
-    )(lens, query, new, key_cache, value_cache)
+        name='update',
+    )(lens, new, key_cache, value_cache)
 
 
 ANY = pl.BlockSpec(memory_space=pl.ANY)
@@ -99,6 +89,7 @@
 
 MESH = pl.DeviceIdType.MESH
 CORES = 2
+EARLY = (2,)
 
 
 class Moves:
@@ -146,7 +137,7 @@
     return pl.ds(pl.multiple_of(start * width, width), width)
 
 
-def query_kernel(side, hid_ref, wq_ref, wo_ref, wk_ref, wv_ref, q_ref, wa_ref, wb_ref, new_ref, wq_all, hid, q_buf, acc, w_new, own_w, load_sems, send_sems, recv_sems):
+def attend_kernel(side, len_ref, hid_ref, wq_ref, wo_ref, wk_ref, wv_ref, k_hbm, v_hbm, wa_ref, wb_ref, new_ref, ctx_ref, wq_all, hid, q_buf, q_got, acc, w_new, own_w, k_ref, v_ref, q_rows, ctx_rows, load_sems, send_sems, recv_sems):
     y, x, c = place(side)
     rows, dim = hid_ref.shape[3:]
     half = wq_ref.shape[1]
@@ -174,12 +165,13 @@
     along = ((x, lambda u: dev(y, u)), (y, lambda u: dev(u, x)))
     wcols = lambda t, u: columns(t * side + u, width)
     for t, (u, at) in enumerate(along):
-        mv.send(('w', t, 2), wo_ref.at[:, wcols(t, step(u, 2))], w_refs[t].at[u, c], at(step(u, 2)))
-        for d in (1, 3):
-            mv.send(('w', t, d), wo_ref.at[:, wcols(t, step(u, d))], w_refs[t].at[u, c], at(step(u, d)))
+        for d in EARLY:
+            mv.send(('w', t, d), wo_ref.at[:, wcols(t, step(u, d))], w_refs[t].at[u], at(step(u, d)))
         mv.local(('w_own', t), wo_ref.at[:, wcols(t, u)], own_w.at[t])
     for j, ref in enumerate((wk_ref, wv_ref)):
         mv.local(('w_new', j), ref, w_new.at[j])
+    for j, (src, dst) in enumerate(((k_hbm, k_ref), (v_hbm, v_ref))):
+        mv.local(('cache', j), src, dst)
 
     def gain(h, core, part):
         acc[h] += jnp.dot(hid[pl.ds(h * pair, pair), :, :, part].reshape(pair * side * rows, depth), wq_all[core, part, :], preferred_element_type=jnp.float32)
@@ -209,35 +201,56 @@
 
     for t, (u, at) in enumerate(along):
         mv.done(('w_own', t))
-        mv.local(('w_put', t), own_w.at[t], w_refs[t].at[u, c])
-        mv.send(('wS', t, 0), own_w.at[t], w_refs[t].at[u, c], other)
+        mv.local(('w_put', t), own_w.at[t], w_refs[t].at[u])
     mv.got('wq')
     for i, dy in enumerate(order):
         if i % pair == 0:
             project(i // pair)
         for dx in [d for d in (2, 1, 3, 0)][:side]:
             if dy or dx:
-                mv.send(('q', dy, dx), q_buf.at[i, step(x, dx)], q_ref.at[y, x], dev(step(y, dy), step(x, dx)))
+                mv.send(('q', dy, dx), q_buf.at[i, step(x, dx)], q_got.at[y, x], dev(step(y, dy), step(x, dx)))
             else:
-                mv.local('q_own', q_buf.at[i, x], q_ref.at[y, x])
+                q_got[y, x] = q_buf[i, x]
+    for t, (u, at) in enumerate(along):
+        for d in range(1, side):
+            if d not in EARLY:
+                mv.send(('w', t, d), wo_ref.at[:, wcols(t, step(u, d))], w_refs[t].at[u], at(step(u, d)))
     for j in range(2):
         mv.done(('w_new', j))
         new = jnp.zeros((rows, w_new.shape[2]), jnp.float32)
         for k in range(0, dim, depth):
             new += jnp.dot(hid[side - 1, x, :, k:k + depth], w_new[j, k:k + depth, :], preferred_element_type=jnp.float32)
         new_ref[j] = new.astype(jnp.bfloat16).astype(jnp.float32)
-    for d in (2, 1, 3):
-        for t, (u, at) in enumerate(along):
-            mv.got(('w', t, d))
-            tile = w_refs[t].at[step(u, -d), c]
-            mv.send(('wS', t, d), tile, tile, other)
+        mv.done(('cache', j))
     for dy, dx in peers:
         mv.got(('q', dy, dx))
-    mv.done('q_own')
+
+    chips, head_dim = side * side, k_ref.shape[2]
+    chunk = min(CHUNK, rows)
+    lanes = [slice(h * head_dim, (h + 1) * head_dim) for h in range(CORES * half // head_dim)]
+    first = lax.axis_index('model') * rows
+
+    @pl.loop(0, rows // chunk)
+    def _(i):
+        part = pl.ds(pl.multiple_of(i * chunk, chunk), chunk)
+        for h, lane in enumerate(lanes):
+            q_rows[h] = q_got[:, :, part, lane].astype(jnp.float32).reshape(chips * chunk, head_dim)
+        some = [i * chunk + r for r in range(chunk)]
+        query = []
+        for r in range(chunk):
+            query.append(jnp.concatenate([q_rows[h, pl.ds(r, chips, stride=chunk), :] for h in range(len(lanes))], axis=0))
+        new_keys, new_values = ([new_ref[j, pl.ds(r, 1), :] for r in some] for j in range(2))
+        out = attend_rows(query, [k_ref[r] for r in some], [v_ref[r] for r in some], new_keys, new_values, [len_ref[first + r] for r in some], head_dim ** -0.5)
+        for r in range(chunk):
+            for h in range(len(lanes)):
+                ctx_rows[h, pl.ds(r, chips, stride=chunk), :] = out[r][h * chips:(h + 1) * chips]
+        for h, lane in enumerate(lanes):
+            ctx_ref[:, :, part, lane] = ctx_rows[h].astype(jnp.bfloat16).reshape(side, side, chunk, head_dim)
+
     for t in range(2):
         mv.done(('w_put', t))
-        for d in range(side):
-            mv.got(('wS', t, d))
+        for d in range(1, side):
+            mv.got(('w', t, d))
     mv.finish()
 
 
@@ -271,7 +284,8 @@
         mv.send(('gL', t, 0), ctx_of(t, v), held.at[t, u, v], at(t, v, step(u, -1)))
     for t in both:
         v, u = spots[t]
-        mv.local(('w', t), (wa_ref, wb_ref)[t], w_buf.at[t])
+        mv.local(('w', t), (wa_ref, wb_ref)[t], w_buf.at[t, :, c])
+        mv.send(('wS', t), (wa_ref, wb_ref)[t], w_buf.at[t, :, c], other)
         mv.local(('hid', t), view(hid_ref, t, v, u), final.at[t])
 
     def spread(t, p, tag):
@@ -302,6 +316,7 @@
         forward(t, 0, 'R')
     for t in both:
         mv.done(('w', t))
+        mv.got(('wS', t))
 
     def product(t, p):
         v, u = spots[t]
@@ -415,29 +430,36 @@
     return [pltpu.SemaphoreType.DMA((n,)), pltpu.SemaphoreType.DMA((n,))]
 
 
-def project_queries(side, hidden, w_query, w_out, w_key, w_value):
+def attend(side, lens, hidden, w_query, w_out, w_key, w_value, key_cache, value_cache):
     rows, dim = hidden.shape[3:]
     half = w_query.shape[1]
     w_rows, width = w_out.shape[0], w_out.shape[1] // (2 * side)
-    bf16 = jnp.bfloat16
-    tile = jax.ShapeDtypeStruct((side, CORES, w_rows, width), bf16)
+    bf16, f32 = jnp.bfloat16, jnp.float32
+    tile = jax.ShapeDtypeStruct((side, w_rows, width), bf16)
+    wide = (side, side, rows, CORES * half)
+    depth = min(2048, dim)
     return pl.pallas_call(
-        functools.partial(query_kernel, side),
-        out_shape=[jax.ShapeDtypeStruct((side, side, rows, CORES * half), bf16), tile, tile, jax.ShapeDtypeStruct((2, rows, w_key.shape[1]), jnp.float32)],
-        in_specs=[ANY] * 5,
-        out_specs=[ANY] * 3 + [VMEM],
+        functools.partial(attend_kernel, side),
+        out_shape=[tile, tile, jax.ShapeDtypeStruct((2, rows, w_key.shape[1]), f32), jax.ShapeDtypeStruct(wide, bf16)],
+        in_specs=[pl.BlockSpec(memory_space=pltpu.SMEM)] + [ANY] * 7,
+        out_specs=[ANY, ANY, VMEM, VMEM],
         scratch_shapes=[
             pltpu.VMEM((CORES, dim, half), bf16),
             pltpu.VMEM((side, side, rows, dim), bf16),
-            pltpu.VMEM((side, side, rows, CORES * half), bf16),
-            pltpu.VMEM((2, side // 2 * side * rows, half), jnp.float32),
+            pltpu.VMEM(wide, bf16),
+            pltpu.VMEM(wide, bf16),
+            pltpu.VMEM((2, side // 2 * side * rows, half), f32),
             pltpu.VMEM((2,) + w_key.shape, bf16),
             pltpu.VMEM((2, w_rows, width), bf16),
-            pltpu.SemaphoreType.DMA((1 + side, dim // min(2048, dim))),
+            pltpu.VMEM(key_cache.shape, bf16),
+            pltpu.VMEM(value_cache.shape, bf16),
+            pltpu.VMEM((CORES * half // w_key.shape[1], side * side * min(CHUNK, rows), w_key.shape[1]), f32),
+            pltpu.VMEM((CORES * half // w_key.shape[1], side * side * min(CHUNK, rows), w_key.shape[1]), f32),
+            pltpu.SemaphoreType.DMA((1 + side, dim // depth)),
         ] + sems(64),
         compiler_params=pltpu.CompilerParams(collective_id=0, has_side_effects=True, vmem_limit_bytes=63 << 20),
-        name='project_queries',
-    )(hidden, w_query, w_out, w_key, w_value)
+        name='attend',
+    )(lens, hidden, w_query, w_out, w_key, w_value, key_cache, value_cache)
 
 
 def project_context(side, context, w_a, w_b, hidden):
@@ -451,7 +473,7 @@
         out_specs=ANY,
         scratch_shapes=[
             pltpu.VMEM((2, side, side, side, rows, depth), bf16),
-            pltpu.VMEM((2,) + w_a.shape, bf16),
+            pltpu.VMEM((2, side, CORES) + w_a.shape[1:], bf16),
             pltpu.VMEM((2, side, rows, width), f32),
             pltpu.VMEM((2, 2, side // 2, rows, width), f32),
             pltpu.VMEM((2, 4, side, rows, width), bf16),
@@ -492,15 +514,11 @@
     def group_step(hidden, w_query, w_key, w_value, w_out, key_cache, value_cache, lengths):
         n_rows, dim = hidden.shape
         local_rows = key_cache.shape[0]
-        head_dim = key_cache.shape[2]
-        chip_cols = CORES * w_query.shape[1]
-        n_heads = side * side * chip_cols // head_dim
         hidden_tiles = hidden.reshape(side, side, CORES, local_rows, dim)
-        query, w_a, w_b, new = project_queries(side, hidden_tiles, w_query, w_out, w_key, w_value)
-        query = query.reshape(side * side, local_rows, chip_cols // head_dim, head_dim).transpose(1, 0, 2, 3).reshape(local_rows, n_heads, head_dim)
-        key_upd, value_upd, context = attend(lengths, query, new, key_cache, value_cache)
-        context = context.reshape(local_rows, side * side, chip_cols // head_dim, head_dim).transpose(1, 0, 2, 3).reshape(side, side, local_rows, chip_cols)
-        hidden_out = put(project_context(side, context, w_a, w_b, hidden_tiles))
+        w_a, w_b, new, context = attend(side, lengths, hidden_tiles, w_query, w_out, w_key, w_value, key_cache, value_cache)
+        key_upd, value_upd = update(lengths, new, key_cache, value_cache)
+        result = project_context(side, context, w_a, w_b, hidden_tiles)
+        hidden_out = put(result)
         return hidden_out.reshape(n_rows, dim), key_upd, value_upd
 
     row_spec = P('replica', None)

time: 242 us -> 235 us (0.971)
  local copies, waits for them, and re-layouts: 5.82 us -> 0 us
    reshape x4 -> x0, local copies, waits for them, and re-layouts: 5.82 us -> none  [the longest x2 2.92 us: group_step(): context.reshape(local_rows, side * side, chip_cols // head_dim, head_dim)]
where the time goes in v4:
time: 235 us
  Pallas kernels  234 us (100%)
    pallas_call x1, Pallas kernels, project_context(): pl.pallas_call(functools.partial(output_kernel, side), out_shape=pltpu.VM...  161 us
    pallas_call x1, Pallas kernels, attend(): pl.pallas_call(functools.partial(attend_kernel, side), out_shape=[tile, t...  50 us
    pallas_call x1, Pallas kernels, update(): pl.pallas_call(update_kernel, in_specs=[pl.BlockSpec(memory_space=pltpu.S...  12 us
    pallas_call x1, Pallas kernels, put(): pl.pallas_call(put_kernel, out_shape=jax.ShapeDtypeStruct(result.shape, r...  11 us

profile of v4, /device:TPU:97, one launch (start us, length us, event | category | flops | bytes accessed | tf_op | source)
XLA Modules:
  0.0 235.0 jit_solution(2710394952430443745)
XLA Ops:
  0.6 50.0 %attend.1 = (bf16[4,256,1024]{2,1,0:T(8,128)(2,1)}, bf16[4,256,1024]{2,1,0:T(8,128)(2,1)}, f32[2,64,128]{2,1,0:T(8,128)}, bf16[4,4,64,512]{3,2,1,0:T(8,128)(2,1)}) custom-call(s32[2048]{0:T(1024)} %len_ref.3, bf16[4,4,2,64,8192]{4,3,2,1,0:T(8,128)(2,1)} %bitcast.2, bf16[8192,256]{1,0:T(8,128)(2,1)} %wq_ref.1, bf16[256,8192]{1,0:T(8,128)(2,1)} %wo_ref.1, ...), custom_call_target="tpu_custom_call" | custom-call | tf_op jit(solution)/shard_map/attend/pallas_call | solution.py:441
  50.6 161.2 %project_context.1.src_ref = bf16[4,4,2,64,8192]{4,3,2,1,0:T(8,128)(2,1)S(1)} custom-call(bf16[4,4,64,512]{3,2,1,0:T(8,128)(2,1)} %get-tuple-element.9.ctx_ref, bf16[4,256,1024]{2,1,0:T(8,128)(2,1)} %get-tuple-element.10.wa_ref, bf16[4,256,1024]{2,1,0:T(8,128)(2,1)} %get-tuple-element.11.wb_ref, bf16[4,4,2,64,8192]{4,3,2,1,0:T(8,128)(2,1)} %bitcast.3), custom_call_target="tpu_custom_call" | custom-call | tf_op jit(solution)/shard_map/project_context/pallas_call | solution.py:469
  211.8 11.0 %put.1 = bf16[4,4,2,64,8192]{4,3,2,1,0:T(8,128)(2,1)} custom-call(bf16[4,4,2,64,8192]{4,3,2,1,0:T(8,128)(2,1)S(1)} %project_context.1.src_ref), custom_call_target="tpu_custom_call" | custom-call | tf_op jit(solution)/shard_map/put/pallas_call | solution.py:500
  222.9 12.0 %update.1 = (bf16[64,512,128]{2,1,0:T(8,128)(2,1)}, bf16[64,512,128]{2,1,0:T(8,128)(2,1)}) custom-call(s32[2048]{0:T(1024)} %len_ref.3, f32[2,64,128]{2,1,0:T(8,128)} %get-tuple-element.12.new_ref, bf16[64,512,128]{2,1,0:T(8,128)(2,1)} %k_hbm.3, bf16[64,512,128]{2,1,0:T(8,128)(2,1)} %v_hbm.3), custom_call_target="tpu_custom_call" | custom-call | tf_op jit(solution)/shard_map/update/pallas_call | solution.py:70

commit v5 on v4

--- a/solution.py
+++ b/solution.py
@@ -26,59 +26,64 @@
     return [(m + o.astype(jnp.bfloat16).astype(jnp.float32) * v) / t for m, o, v, t in zip(mixed, own, new_values, sums)]
 
 
-def update_kernel(len_ref, new_ref, k_hbm, v_hbm, ko_hbm, vo_hbm, k_ref, v_ref, in_sems, out_sems):
+def update_kernel(len_ref, new_ref, k_ref, v_ref, ko_hbm, vo_hbm, tiles, big_sems, small_sems):
     n, seq_len, head_dim = k_ref.shape
     tile = math.gcd(seq_len, 16)
     first = lax.axis_index('model') * n
-
-    def loads(i):
+    pairs = ((k_ref, ko_hbm), (v_ref, vo_hbm))
+
+    def bulk(i):
         part = pl.ds(i * CHUNK, CHUNK)
-        return [pltpu.make_async_copy(src.at[part], dst.at[part], in_sems.at[j, i]) for j, (src, dst) in enumerate(((k_hbm, k_ref), (v_hbm, v_ref)))]
-
-    def stores(i):
-        part = pl.ds(i * CHUNK, CHUNK)
-        return [pltpu.make_async_copy(src.at[part], dst.at[part], out_sems.at[j, i]) for j, (src, dst) in enumerate(((k_ref, ko_hbm), (v_ref, vo_hbm)))]
+        return [pltpu.make_async_copy(src.at[part], dst.at[part], big_sems.at[j, i]) for j, (src, dst) in enumerate(pairs)]
+
+    def start_of(r):
+        return pl.multiple_of((len_ref[first + r] // tile) * tile, tile)
+
+    def patches(r):
+        return [pltpu.make_async_copy(tiles.at[j, r], dst.at[r, pl.ds(start_of(r), tile)], small_sems.at[j, r]) for j, (_, dst) in enumerate(pairs)]
 
     for i in range(n // CHUNK):
-        for copy in loads(i):
+        for copy in bulk(i):
             copy.start()
 
     @pl.loop(0, n // CHUNK)
     def _(i):
-        for copy in loads(i):
+        for r in range(CHUNK):
+            r = i * CHUNK + r
+            base = start_of(r)
+            pick = lax.broadcasted_iota(jnp.int32, (tile, head_dim), 0) == len_ref[first + r] - base
+            for j, (ref, _) in enumerate(pairs):
+                new = jnp.broadcast_to(new_ref[j, pl.ds(r, 1), :], (tile, head_dim))
+                old = ref[r, pl.ds(base, tile), :].astype(jnp.float32)
+                tiles[j, r] = jnp.where(pick, new, old).astype(jnp.bfloat16)
+
+    @pl.loop(0, n // CHUNK)
+    def _(i):
+        for copy in bulk(i):
             copy.wait()
         for r in range(CHUNK):
-            r = i * CHUNK + r
-            row_len = len_ref[first + r]
-            base = pl.multiple_of((row_len // tile) * tile, tile)
-            pick = lax.broadcasted_iota(jnp.int32, (tile, head_dim), 0) == row_len - base
-            for j, ref in enumerate((k_ref, v_ref)):
-                new = jnp.broadcast_to(new_ref[j, pl.ds(r, 1), :], (tile, head_dim))
-                old = ref[r, pl.ds(base, tile), :].astype(jnp.float32)
-                ref[r, pl.ds(base, tile), :] = jnp.where(pick, new, old).astype(jnp.bfloat16)
-        for copy in stores(i):
-            copy.start()
-
-    @pl.loop(0, n // CHUNK)
-    def _(i):
-        for copy in stores(i):
+            for copy in patches(i * CHUNK + r):
+                copy.start()
+
+    @pl.loop(0, n)
+    def _(r):
+        for copy in patches(r):
             copy.wait()
 
 
 def update(lens, new, key_cache, value_cache):
-    n = key_cache.shape[0]
+    n, seq_len, head_dim = key_cache.shape
     return pl.pallas_call(
         update_kernel,
-        in_specs=[pl.BlockSpec(memory_space=pltpu.SMEM), VMEM, ANY, ANY],
+        in_specs=[pl.BlockSpec(memory_space=pltpu.SMEM), VMEM, VMEM, VMEM],
         out_specs=[ANY] * 2,
         out_shape=[jax.ShapeDtypeStruct(x.shape, x.dtype) for x in (key_cache, value_cache)],
         scratch_shapes=[
-            pltpu.VMEM(key_cache.shape, jnp.bfloat16),
-            pltpu.VMEM(value_cache.shape, jnp.bfloat16),
+            pltpu.VMEM((2, n, math.gcd(seq_len, 16), head_dim), jnp.bfloat16),
             pltpu.SemaphoreType.DMA((2, n // CHUNK)),
-            pltpu.SemaphoreType.DMA((2, n // CHUNK)),
+            pltpu.SemaphoreType.DMA((2, n)),
         ],
-        compiler_params=pltpu.CompilerParams(vmem_limit_bytes=63 << 20),
+        compiler_params=pltpu.CompilerParams(vmem_limit_bytes=2 << 20),
         name='update',
     )(lens, new, key_cache, value_cache)
 
@@ -137,7 +142,7 @@
     return pl.ds(pl.multiple_of(start * width, width), width)
 
 
-def attend_kernel(side, len_ref, hid_ref, wq_ref, wo_ref, wk_ref, wv_ref, k_hbm, v_hbm, wa_ref, wb_ref, new_ref, ctx_ref, wq_all, hid, q_buf, q_got, acc, w_new, own_w, k_ref, v_ref, q_rows, ctx_rows, load_sems, send_sems, recv_sems):
+def attend_kernel(side, len_ref, hid_ref, wq_ref, wo_ref, wk_ref, wv_ref, k_hbm, v_hbm, wa_ref, wb_ref, new_ref, ctx_ref, k_ref, v_ref, wq_all, hid, q_buf, q_got, acc, w_new, own_w, q_rows, ctx_rows, load_sems, send_sems, recv_sems):
     y, x, c = place(side)
     rows, dim = hid_ref.shape[3:]
     half = wq_ref.shape[1]
@@ -150,7 +155,8 @@
     peers = [(dy, dx) for dy in range(side) for dx in range(side) if dy or dx]
     mv = Moves(send_sems, recv_sems)
     order = list(range(1, side)) + [0]
-    depth, pair = min(2048, dim), side // 2
+    depth, piece = min(2048, dim), rows // 2
+    halves = [pl.ds(h * piece, piece) for h in range(2)]
 
     def loads(k):
         part = columns(k, depth)
@@ -174,10 +180,10 @@
         mv.local(('cache', j), src, dst)
 
     def gain(h, core, part):
-        acc[h] += jnp.dot(hid[pl.ds(h * pair, pair), :, :, part].reshape(pair * side * rows, depth), wq_all[core, part, :], preferred_element_type=jnp.float32)
+        acc[h] += jnp.dot(hid[:, :, halves[h], part].reshape(side * side * piece, depth), wq_all[core, part, :], preferred_element_type=jnp.float32)
 
     def store(h, core):
-        q_buf[pl.ds(h * pair, pair), :, :, columns(core, half)] = acc[h].astype(jnp.bfloat16).reshape(pair, side, rows, half)
+        q_buf[:, :, halves[h], columns(core, half)] = acc[h].astype(jnp.bfloat16).reshape(side, side, piece, half)
         acc[h] = jnp.zeros_like(acc[h])
 
     acc[...] = jnp.zeros_like(acc)
@@ -203,14 +209,14 @@
         mv.done(('w_own', t))
         mv.local(('w_put', t), own_w.at[t], w_refs[t].at[u])
     mv.got('wq')
-    for i, dy in enumerate(order):
-        if i % pair == 0:
-            project(i // pair)
-        for dx in [d for d in (2, 1, 3, 0)][:side]:
-            if dy or dx:
-                mv.send(('q', dy, dx), q_buf.at[i, step(x, dx)], q_got.at[y, x], dev(step(y, dy), step(x, dx)))
-            else:
-                q_got[y, x] = q_buf[i, x]
+    for h, some in enumerate(halves):
+        project(h)
+        for i, dy in enumerate(order):
+            for dx in (2, 1, 3, 0):
+                if dy or dx:
+                    mv.send(('q', dy, dx, h), q_buf.at[i, step(x, dx), some], q_got.at[y, x, some], dev(step(y, dy), step(x, dx)))
+                else:
+                    q_got[y, x, some] = q_buf[i, x, some]
     for t, (u, at) in enumerate(along):
         for d in range(1, side):
             if d not in EARLY:
@@ -222,16 +228,13 @@
             new += jnp.dot(hid[side - 1, x, :, k:k + depth], w_new[j, k:k + depth, :], preferred_element_type=jnp.float32)
         new_ref[j] = new.astype(jnp.bfloat16).astype(jnp.float32)
         mv.done(('cache', j))
-    for dy, dx in peers:
-        mv.got(('q', dy, dx))
 
     chips, head_dim = side * side, k_ref.shape[2]
-    chunk = min(CHUNK, rows)
+    chunk = min(CHUNK, piece)
     lanes = [slice(h * head_dim, (h + 1) * head_dim) for h in range(CORES * half // head_dim)]
     first = lax.axis_index('model') * rows
 
-    @pl.loop(0, rows // chunk)
-    def _(i):
+    def attend_chunk(i):
         part = pl.ds(pl.multiple_of(i * chunk, chunk), chunk)
         for h, lane in enumerate(lanes):
             q_rows[h] = q_got[:, :, part, lane].astype(jnp.float32).reshape(chips * chunk, head_dim)
@@ -246,6 +249,11 @@
                 ctx_rows[h, pl.ds(r, chips, stride=chunk), :] = out[r][h * chips:(h + 1) * chips]
         for h, lane in enumerate(lanes):
             ctx_ref[:, :, part, lane] = ctx_rows[h].astype(jnp.bfloat16).reshape(side, side, chunk, head_dim)
+
+    for h in range(2):
+        for dy, dx in peers:
+            mv.got(('q', dy, dx, h))
+        pl.loop(h * piece // chunk, (h + 1) * piece // chunk)(attend_chunk)
 
     for t in range(2):
         mv.done(('w_put', t))
@@ -440,9 +448,9 @@
     depth = min(2048, dim)
     return pl.pallas_call(
         functools.partial(attend_kernel, side),
-        out_shape=[tile, tile, jax.ShapeDtypeStruct((2, rows, w_key.shape[1]), f32), jax.ShapeDtypeStruct(wide, bf16)],
+        out_shape=[tile, tile, jax.ShapeDtypeStruct((2, rows, w_key.shape[1]), f32), jax.ShapeDtypeStruct(wide, bf16), pltpu.VMEM(key_cache.shape, bf16), pltpu.VMEM(value_cache.shape, bf16)],
         in_specs=[pl.BlockSpec(memory_space=pltpu.SMEM)] + [ANY] * 7,
-        out_specs=[ANY, ANY, VMEM, VMEM],
+        out_specs=[ANY, ANY, VMEM, VMEM, VMEM, VMEM],
         scratch_shapes=[
             pltpu.VMEM((CORES, dim, half), bf16),
             pltpu.VMEM((side, side, rows, dim), bf16),
@@ -451,13 +459,11 @@
             pltpu.VMEM((2, side // 2 * side * rows, half), f32),
             pltpu.VMEM((2,) + w_key.shape, bf16),
             pltpu.VMEM((2, w_rows, width), bf16),
-            pltpu.VMEM(key_cache.shape, bf16),
-            pltpu.VMEM(value_cache.shape, bf16),
-            pltpu.VMEM((CORES * half // w_key.shape[1], side * side * min(CHUNK, rows), w_key.shape[1]), f32),
-            pltpu.VMEM((CORES * half // w_key.shape[1], side * side * min(CHUNK, rows), w_key.shape[1]), f32),
+            pltpu.VMEM((CORES * half // w_key.shape[1], side * side * min(CHUNK, rows // 2), w_key.shape[1]), f32),
+            pltpu.VMEM((CORES * half // w_key.shape[1], side * side * min(CHUNK, rows // 2), w_key.shape[1]), f32),
             pltpu.SemaphoreType.DMA((1 + side, dim // depth)),
         ] + sems(64),
-        compiler_params=pltpu.CompilerParams(collective_id=0, has_side_effects=True, vmem_limit_bytes=63 << 20),
+        compiler_params=pltpu.CompilerParams(collective_id=0, has_side_effects=True, vmem_limit_bytes=40 << 20),
         name='attend',
     )(lens, hidden, w_query, w_out, w_key, w_value, key_cache, value_cache)
 
@@ -515,8 +521,9 @@
         n_rows, dim = hidden.shape
         local_rows = key_cache.shape[0]
         hidden_tiles = hidden.reshape(side, side, CORES, local_rows, dim)
-        w_a, w_b, new, context = attend(side, lengths, hidden_tiles, w_query, w_out, w_key, w_value, key_cache, value_cache)
-        key_upd, value_upd = update(lengths, new, key_cache, value_cache)
+        w_a, w_b, new, context, keys, values = attend(side, lengths, hidden_tiles, w_query, w_out, w_key, w_value, key_cache, value_cache)
+        key_upd, value_upd = update(lengths, new, keys, values)
+        context, key_upd, value_upd = lax.optimization_barrier((context, key_upd, value_upd))
         result = project_context(side, context, w_a, w_b, hidden_tiles)
         hidden_out = put(result)
         return hidden_out.reshape(n_rows, dim), key_upd, value_upd

time: 235 us -> 234 us (level)
    pallas_call x1, Pallas kernels: 12 us -> 8.59 us  [update(): pl.pallas_call(update_kernel, in_specs=[pl.BlockSpec(memory_space=pltpu.S...]
where the time goes in v5:
time: 234 us; the launch traced here: 233 us
  Pallas kernels  232 us (99%)
    pallas_call x1, Pallas kernels, project_context(): pl.pallas_call(functools.partial(output_kernel, side), out_shape=pltpu.VM...  163 us
    pallas_call x1, Pallas kernels, attend(): pl.pallas_call(functools.partial(attend_kernel, side), out_shape=[tile, t...  49.5 us
    pallas_call x1, Pallas kernels, put(): pl.pallas_call(put_kernel, out_shape=jax.ShapeDtypeStruct(result.shape, r...  11 us
    pallas_call x1, Pallas kernels, update(): pl.pallas_call(update_kernel, in_specs=[pl.BlockSpec(memory_space=pltpu.S...  8.59 us

profile of v5, /device:TPU:97, one launch (start us, length us, event | category | flops | bytes accessed | tf_op | source)
XLA Modules:
  0.0 233.4 jit_solution(17202850023174972551)
XLA Ops:
  0.6 0.0 copy-start.1
  0.6 49.5 %attend.1 = (bf16[4,256,1024]{2,1,0:T(8,128)(2,1)}, bf16[4,256,1024]{2,1,0:T(8,128)(2,1)}, f32[2,64,128]{2,1,0:T(8,128)}, bf16[4,4,64,512]{3,2,1,0:T(8,128)(2,1)...) custom-call(s32[2048]{0:T(1024)} %len_ref.3, bf16[4,4,2,64,8192]{4,3,2,1,0:T(8,128)(2,1)} %bitcast.2, ...), custom_call_target="tpu_custom_call" | custom-call | tf_op jit(solution)/shard_map/attend/pallas_call | solution.py:449
  50.2 0.0 copy-done.1
  50.2 0.0 copy-start
  50.2 0.8 copy-done
  51.0 8.6 %update.1 = (bf16[64,512,128]{2,1,0:T(8,128)(2,1)}, bf16[64,512,128]{2,1,0:T(8,128)(2,1)}) custom-call(s32[2048]{0:T(1024)S(1)} %copy-done.1, f32[2,64,128]{2,1,0:T(8,128)S(1)} %copy-done, bf16[64,512,128]{2,1,0:T(8,128)(2,1)S(1)} %get-tuple-element.16.k_ref, bf16[64,512,128]{2,1,0:T(8,128)(2,1)S(1)} %get-tuple-element.17.v_ref), custom_call_target="tpu_custom_call" | custom-call | tf_op jit(solution)/shard_map/update/pallas_call | solution.py:76
  59.6 162.5 %project_context.1.src_ref = bf16[4,4,2,64,8192]{4,3,2,1,0:T(8,128)(2,1)S(1)} custom-call(bf16[4,4,64,512]{3,2,1,0:T(8,128)(2,1)} %get-tuple-element.20.ctx_ref, bf16[4,256,1024]{2,1,0:T(8,128)(2,1)} %get-tuple-element.21.wa_ref, bf16[4,256,1024]{2,1,0:T(8,128)(2,1)} %get-tuple-element.22.wb_ref, bf16[4,4,2,64,8192]{4,3,2,1,0:T(8,128)(2,1)} %bitcast.3), custom_call_target="tpu_custom_call" | custom-call | tf_op jit(solution)/shard_map/project_context/pallas_call | solution.py:475
  222.2 11.0 %put.1 = bf16[4,4,2,64,8192]{4,3,2,1,0:T(8,128)(2,1)} custom-call(bf16[4,4,2,64,8192]{4,3,2,1,0:T(8,128)(2,1)S(1)} %project_context.1.src_ref), custom_call_target="tpu_custom_call" | custom-call | tf_op jit(solution)/shard_map/put/pallas_call | solution.py:506
Async XLA Ops:
  0.6 49.6 %copy-start.1 = (s32[2048]{0:T(1024)S(1)}, s32[2048]{0:T(1024)}, u32[]{:S(2)}) copy-start(s32[2048]{0:T(1024)} %len_ref.3) | copy-start | bytes 24580
  50.2 0.8 copy-start

commit v6 on v5

--- a/solution.py
+++ b/solution.py
@@ -94,7 +94,6 @@
 
 MESH = pl.DeviceIdType.MESH
 CORES = 2
-EARLY = (2,)
 
 
 class Moves:
@@ -142,7 +141,7 @@
     return pl.ds(pl.multiple_of(start * width, width), width)
 
 
-def attend_kernel(side, len_ref, hid_ref, wq_ref, wo_ref, wk_ref, wv_ref, k_hbm, v_hbm, wa_ref, wb_ref, new_ref, ctx_ref, k_ref, v_ref, wq_all, hid, q_buf, q_got, acc, w_new, own_w, q_rows, ctx_rows, load_sems, send_sems, recv_sems):
+def attend_kernel(side, len_ref, hid_ref, wq_ref, wo_ref, wk_ref, wv_ref, k_hbm, v_hbm, wa_ref, wb_ref, new_ref, ctx_ref, k_ref, v_ref, wq_all, hid, q_buf, q_got, acc, relay, w_new, own_w, q_rows, ctx_rows, load_sems, send_sems, recv_sems):
     y, x, c = place(side)
     rows, dim = hid_ref.shape[3:]
     half = wq_ref.shape[1]
@@ -170,9 +169,10 @@
     mv.send('wq', wq_ref, wq_all.at[c], other)
     along = ((x, lambda u: dev(y, u)), (y, lambda u: dev(u, x)))
     wcols = lambda t, u: columns(t * side + u, width)
+    top, low = pl.ds(0, w_rows // 2), pl.ds(w_rows // 2, w_rows // 2)
     for t, (u, at) in enumerate(along):
-        for d in EARLY:
-            mv.send(('w', t, d), wo_ref.at[:, wcols(t, step(u, d))], w_refs[t].at[u], at(step(u, d)))
+        mv.send(('w1R', t), wo_ref.at[top, wcols(t, step(u, 2))], relay.at[t, 0], at(step(u, 1)))
+        mv.send(('w1L', t), wo_ref.at[low, wcols(t, step(u, 2))], relay.at[t, 1], at(step(u, -1)))
         mv.local(('w_own', t), wo_ref.at[:, wcols(t, u)], own_w.at[t])
     for j, ref in enumerate((wk_ref, wv_ref)):
         mv.local(('w_new', j), ref, w_new.at[j])
@@ -208,6 +208,10 @@
     for t, (u, at) in enumerate(along):
         mv.done(('w_own', t))
         mv.local(('w_put', t), own_w.at[t], w_refs[t].at[u])
+        mv.got(('w1R', t))
+        mv.send(('w2R', t), relay.at[t, 0], w_refs[t].at[step(u, -1), top], at(step(u, 1)))
+        mv.got(('w1L', t))
+        mv.send(('w2L', t), relay.at[t, 1], w_refs[t].at[step(u, 1), low], at(step(u, -1)))
     mv.got('wq')
     for h, some in enumerate(halves):
         project(h)
@@ -218,9 +222,8 @@
                 else:
                     q_got[y, x, some] = q_buf[i, x, some]
     for t, (u, at) in enumerate(along):
-        for d in range(1, side):
-            if d not in EARLY:
-                mv.send(('w', t, d), wo_ref.at[:, wcols(t, step(u, d))], w_refs[t].at[u], at(step(u, d)))
+        for d in (1, 3):
+            mv.send(('w', t, d), wo_ref.at[:, wcols(t, step(u, d))], w_refs[t].at[u], at(step(u, d)))
     for j in range(2):
         mv.done(('w_new', j))
         new = jnp.zeros((rows, w_new.shape[2]), jnp.float32)
@@ -257,8 +260,8 @@
 
     for t in range(2):
         mv.done(('w_put', t))
-        for d in range(1, side):
-            mv.got(('w', t, d))
+        for key in (('w2R', t), ('w2L', t), ('w', t, 1), ('w', t, 3)):
+            mv.got(key)
     mv.finish()
 
 
@@ -457,6 +460,7 @@
             pltpu.VMEM(wide, bf16),
             pltpu.VMEM(wide, bf16),
             pltpu.VMEM((2, side // 2 * side * rows, half), f32),
+            pltpu.VMEM((2, 2, w_rows // 2, width), bf16),
             pltpu.VMEM((2,) + w_key.shape, bf16),
             pltpu.VMEM((2, w_rows, width), bf16),
             pltpu.VMEM((CORES * half // w_key.shape[1], side * side * min(CHUNK, rows // 2), w_key.shape[1]), f32),

time: 234 us -> 231 us (0.987)
  Pallas kernels: 232 us -> 229 us
    pallas_call x1, Pallas kernels: 49.5 us -> 46.5 us  [attend(): pl.pallas_call(functools.partial(attend_kernel, side), out_shape=[tile, t...]
where the time goes in v6:
time: 231 us
  Pallas kernels  229 us (99%)
    pallas_call x1, Pallas kernels, project_context(): pl.pallas_call(functools.partial(output_kernel, side), out_shape=pltpu.VM...  163 us
    pallas_call x1, Pallas kernels, attend(): pl.pallas_call(functools.partial(attend_kernel, side), out_shape=[tile, t...  46.5 us
    pallas_call x1, Pallas kernels, put(): pl.pallas_call(put_kernel, out_shape=jax.ShapeDtypeStruct(result.shape, r...  11 us
    pallas_call x1, Pallas kernels, update(): pl.pallas_call(update_kernel, in_specs=[pl.BlockSpec(memory_space=pltpu.S...  8.59 us

profile of v6, /device:TPU:97, one launch (start us, length us, event | category | flops | bytes accessed | tf_op | source)
XLA Modules:
  0.0 231.1 jit_solution(4015106168626524148)
XLA Ops:
  0.6 0.0 copy-start.1
  0.6 46.5 %attend.1 = (bf16[4,256,1024]{2,1,0:T(8,128)(2,1)}, bf16[4,256,1024]{2,1,0:T(8,128)(2,1)}, f32[2,64,128]{2,1,0:T(8,128)}, bf16[4,4,64,512]{3,2,1,0:T(8,128)(2,1)...) custom-call(s32[2048]{0:T(1024)} %len_ref.3, bf16[4,4,2,64,8192]{4,3,2,1,0:T(8,128)(2,1)} %bitcast.2, ...), custom_call_target="tpu_custom_call" | custom-call | tf_op jit(solution)/shard_map/attend/pallas_call | solution.py:452
  47.1 0.0 copy-done.1
  47.1 0.0 copy-start
  47.1 0.8 copy-done
  48.0 8.6 %update.1 = (bf16[64,512,128]{2,1,0:T(8,128)(2,1)}, bf16[64,512,128]{2,1,0:T(8,128)(2,1)}) custom-call(s32[2048]{0:T(1024)S(1)} %copy-done.1, f32[2,64,128]{2,1,0:T(8,128)S(1)} %copy-done, bf16[64,512,128]{2,1,0:T(8,128)(2,1)S(1)} %get-tuple-element.16.k_ref, bf16[64,512,128]{2,1,0:T(8,128)(2,1)S(1)} %get-tuple-element.17.v_ref), custom_call_target="tpu_custom_call" | custom-call | tf_op jit(solution)/shard_map/update/pallas_call | solution.py:76
  56.6 163.3 %project_context.1.src_ref = bf16[4,4,2,64,8192]{4,3,2,1,0:T(8,128)(2,1)S(1)} custom-call(bf16[4,4,64,512]{3,2,1,0:T(8,128)(2,1)} %get-tuple-element.20.ctx_ref, bf16[4,256,1024]{2,1,0:T(8,128)(2,1)} %get-tuple-element.21.wa_ref, bf16[4,256,1024]{2,1,0:T(8,128)(2,1)} %get-tuple-element.22.wb_ref, bf16[4,4,2,64,8192]{4,3,2,1,0:T(8,128)(2,1)} %bitcast.3), custom_call_target="tpu_custom_call" | custom-call | tf_op jit(solution)/shard_map/project_context/pallas_call | solution.py:479
  219.9 11.0 %put.1 = bf16[4,4,2,64,8192]{4,3,2,1,0:T(8,128)(2,1)} custom-call(bf16[4,4,2,64,8192]{4,3,2,1,0:T(8,128)(2,1)S(1)} %project_context.1.src_ref), custom_call_target="tpu_custom_call" | custom-call | tf_op jit(solution)/shard_map/put/pallas_call | solution.py:510
Async XLA Ops:
  0.6 46.5 %copy-start.1 = (s32[2048]{0:T(1024)S(1)}, s32[2048]{0:T(1024)}, u32[]{:S(2)}) copy-start(s32[2048]{0:T(1024)} %len_ref.3) | copy-start | bytes 24580
  47.1 0.8 copy-start
